TPU v7x, 128 devices: a whole 4x4x4 slice. The times are simulated.
128 devices in a mesh: circ: 32 (over x_hi, y, z), side: 4 (over x_lo, core).
Axes of the slice: x: 4 (x_hi: 2, x_lo: 2; x = x_hi * 2 + x_lo), y: 4, z: 4, core: 2. Of those that a mesh axis runs over, the one named last changes fastest.
Arguments:
- field: float32 [4, 7, 7, 7, 8, 4096], P('side', None, None, None, None, 'circ'), may hold values from -6 to 6
- coeffs: float32 [4, 3, 7, 7, 7, 8, 4096], P('side', None, None, None, None, None, 'circ'), may hold values from 0.25 to 1.5
- reaction: float32 [4, 7, 7, 7, 8, 4096], P('side', None, None, None, None, 'circ'), may hold values from 0.25 to 8
- step_scale: float32 [4, 7, 7, 7, 8, 4096], P('side', None, None, None, None, 'circ'), may hold values from 0.0001 to 0.0003
- rotation: int32 [4], replicated, may hold values from 0 to 12287
Outputs:
- advanced: float32 [4, 7, 7, 7, 8, 4096], P('side', None, None, None, None, 'circ')
Inputs may be any that keep to these rules, and one draw needn't show every extreme that they name: `rotation`: rotor position in units of one 3-th of an element's circumferential width.
All inputs are finite; a program needn't handle non-finite values.
Results may differ from a plain program's by a relative error of at most 0.0001.
Values sent between devices are 32-bit elements; how exact they have to be, the bound alone decides.
A program may use at most 128 MiB of HBM per device.

v0:
```python
from functools import partial

import jax
import jax.numpy as jnp
import numpy as np
from jax import lax
from jax.sharding import PartitionSpec as P

SUBSTEPS = 3
STEPS = 4


def passed_along(value, axis, steps):
    count = lax.axis_size(axis)
    pairs = [(source, (source + steps) % count) for source in range(count)]
    return lax.ppermute(value, axis, pairs)


def padded_2(block, sides, width, periodic):
    for axis, dim in sides:
        count = lax.axis_size(axis)
        forward = [(i, i + 1) for i in range(count - 1)]
        if periodic:
            forward.append((count - 1, 0))
        backward = [(target, source) for source, target in forward]
        low = lax.ppermute(
            lax.slice_in_dim(block, block.shape[dim] - width, None, axis=dim), axis, forward
        )
        high = lax.ppermute(lax.slice_in_dim(block, 0, width, axis=dim), axis, backward)
        block = jnp.concatenate([low, block, high], axis=dim)
    return block


def gll_points():
    return np.array(
        [
            -1.0,
            -0.830223896278567,
            -0.4688487934707142,
            0.0,
            0.4688487934707142,
            0.830223896278567,
            1.0,
        ]
    )


def derivative_table():
    points = gll_points()
    node_count = points.shape[0]
    weights = np.array(
        [
            1.0 / np.prod([points[j] - points[k] for k in range(node_count) if k != j])
            for j in range(node_count)
        ]
    )
    derivative = np.zeros((node_count, node_count))
    for i in range(node_count):
        for j in range(node_count):
            if i != j:
                derivative[i, j] = weights[j] / weights[i] / (points[i] - points[j])
        derivative[i, i] = -np.sum(derivative[i])
    return derivative


def lagrange_rows(locations):
    points = gll_points()
    identity_mask = np.eye(7) > 0.5
    differences = np.array(
        [[1.0 if q == n else points[n] - points[q] for q in range(7)] for n in range(7)]
    )
    denominator = np.prod(differences, axis=1)
    distances = locations[:, None] - jnp.asarray(points, jnp.float32)[None, :]
    factors = jnp.where(identity_mask[None, :, :], 1.0, distances[:, None, :])
    return jnp.prod(factors, axis=2) / jnp.asarray(denominator, jnp.float32)[None, :]


def mortar_tables(fraction):
    heights = (1.0 + jnp.asarray(gll_points(), jnp.float32)) * 0.5
    on_right = heights >= fraction
    shifted_height = jnp.where(on_right, heights - fraction, heights - fraction + 1.0)
    values = lagrange_rows(2.0 * shifted_height - 1.0)
    from_right = jnp.where(on_right[:, None], values, 0.0)
    from_left = jnp.where(on_right[:, None], 0.0, values)
    return (from_left, from_right)


def element_apply(field, coeffs, reaction):
    derivative = jnp.asarray(derivative_table(), jnp.float32)
    highest = lax.Precision.HIGHEST
    grad_axial = jnp.einsum("pa,arcxe->prcxe", derivative, field, precision=highest)
    grad_radial = jnp.einsum("pr,arcxe->apcxe", derivative, field, precision=highest)
    grad_circ = jnp.einsum("pc,arcxe->arpxe", derivative, field, precision=highest)
    result = reaction * field
    result = result + jnp.einsum(
        "pa,prcxe->arcxe", derivative, coeffs[0] * grad_axial, precision=highest
    )
    result = result + jnp.einsum(
        "pr,apcxe->arcxe", derivative, coeffs[1] * grad_radial, precision=highest
    )
    result = result + jnp.einsum(
        "pc,arpxe->arcxe", derivative, coeffs[2] * grad_circ, precision=highest
    )
    return result


def fixed_pair(hops, circ_count, is_stator, data):
    ahead = passed_along(data, "circ", hops)
    behind = passed_along(data, "circ", (circ_count - hops - 1) % circ_count)
    return jnp.where(is_stator, ahead, behind)


def rotate_window(block, amount, whole_k, is_stator):
    edge_count = block.shape[-1]
    circ_count = lax.axis_size("circ")
    within = amount % edge_count
    sector_k = whole_k // edge_count
    branches = [partial(fixed_pair, hops, circ_count, is_stator) for hops in range(circ_count)]
    rotated = lax.switch(sector_k, branches, block)
    before = passed_along(rotated, "circ", 1)
    joined = jnp.concatenate([before, rotated], axis=3)
    first_index = edge_count - within - 1
    return lax.dynamic_slice_in_dim(joined, first_index, edge_count + 1, 3)


def project_mortar(incoming, amount, whole_k, is_stator, first_table, second_table):
    highest = lax.Precision.HIGHEST
    window = rotate_window(incoming, amount, whole_k, is_stator)
    edge_count = incoming.shape[-1]
    result = jnp.einsum(
        "mn,rnxe->rmxe", first_table, window[:, :, :, :edge_count], precision=highest
    )
    return result + jnp.einsum(
        "mn,rnxe->rmxe", second_table, window[:, :, :, 1:], precision=highest
    )


def local(field, coeffs, reaction, step_scale, rotation):
    side_index = lax.axis_index("side")
    lower = lax.axis_size("side") // 2 - 1
    cycle_length = field.shape[-1] * lax.axis_size("circ")
    is_stator = side_index > lower
    current = field[0]
    for step in range(STEPS):
        applied = element_apply(current, coeffs[0], reaction[0])
        zero_row = jnp.zeros_like(applied[:, 0, :, :1])
        summed = applied.at[:, 6].add(jnp.concatenate([applied[:, 0, :, 1:], zero_row], axis=2))
        summed = summed.at[:, 0].add(jnp.concatenate([zero_row, applied[:, 6, :, :-1]], axis=2))
        sector_rims = jnp.stack([applied[:, :, 0], applied[:, :, 6]])
        padded = padded_2(sector_rims, (("circ", 4),), 1, True)
        summed = summed.at[:, :, 6].add(padded[0, :, :, :, 2:])
        summed = summed.at[:, :, 0].add(padded[1, :, :, :, :-2])
        axial_faces = jnp.stack([applied[0], applied[6]])
        layered = padded_2(axial_faces, (("side", 0),), 1, False)
        below_top = layered[0]
        above_bottom = layered[3]
        offset = rotation[step]
        whole_k = offset // SUBSTEPS
        fraction = (offset % SUBSTEPS).astype(jnp.float32) / SUBSTEPS
        from_left, from_right = mortar_tables(fraction)
        first_table = jnp.where(is_stator, from_left, from_right.T)
        second_table = jnp.where(is_stator, from_right, from_left.T)
        amount = jnp.where(is_stator, whole_k, cycle_length - whole_k - 1)
        incoming = jnp.where(is_stator, below_top, above_bottom)
        contribution = project_mortar(
            incoming, amount, whole_k, is_stator, first_table, second_table
        )
        bottom_add = jnp.where(side_index == lower + 1, contribution, below_top)
        top_add = jnp.where(side_index == lower, contribution, above_bottom)
        summed = summed.at[0].add(bottom_add)
        summed = summed.at[6].add(top_add)
        current = current - step_scale[0] * summed
    return current[None]


def solution(mesh):
    in_specs = (
        P("side", None, None, None, None, "circ"),
        P("side", None, None, None, None, None, "circ"),
        P("side", None, None, None, None, "circ"),
        P("side", None, None, None, None, "circ"),
        P(),
    )
    out_specs = P("side", None, None, None, None, "circ")
    return jax.shard_map(local, mesh=mesh, in_specs=in_specs, out_specs=out_specs, check_vma=False)
```

profile of v0, /device:TPU:1, one launch (start us, length us, event | category | flops | bytes accessed | tf_op | source)
XLA Modules:
  0.0 328.2 jit_solution(18327385688843211976)
XLA Ops:
  0.0 3.1 fusion.64
  6.6 2.0 fusion.28
  13.7 3.3 collective-permute-start.259
  16.9 3.3 %collective-permute-start.258 = (f32[1,7,7,8,128]{4,3,2,1,0:T(8,128)}, f32[1,7,7,8,128]{4,3,2,1,0:T(8,128)S(1)}, u32[]{:S(2)}, u32[]{:S(2)}) collective-permute-start(f32[1,7,7,8,128]{4,3,2,1,0:T(8,128)} %get-tuple-element.1837), channel_id=1, source_target_pairs={{0,1},{1,2},{2,3},{4,5},{5,6},{6,7},{8,9},{9,10},{10,11},{12,13},{... | collective-permute-start | bytes 602120 | tf_op jit(solution)/shard_map/ppermute | solution.py:26
  23.7 7.0 %collective-permute-start.256 = (f32[2,7,7,8,1]{4,3,2,1,0:T(8,128)}, f32[2,7,7,8,1]{4,3,2,1,0:T(8,128)}, u32[]{:S(2)}, u32[]{:S(2)}) collective-permute-start(f32[2,7,7,8,1]{4,3,2,1,0:T(8,128)} %get-tuple-element.1849), channel_id=1, source_target_pairs={{4,0},{8,4},{12,8},{16,12},{20,16},{24,20},{28,24},{32,28},{36,32}... | collective-permute-start | bytes 9416 | tf_op jit(solution)/shard_map/ppermute | solution.py:29
  44.4 1.9 fusion.131
  46.3 2.6 copy.229
  48.9 27.3 %conditional.4 = (pred[]{:T(512)}, f32[7,7,8,128]{3,1,2,0:T(8,128)S(1)}, f32[7,7,8,128]{3,1,2,0:T(8,128)S(1)}) conditional(s32[]{:T(128)} %clamp.12, (pred[]{:T(512)}, pred[]{:T(512)}, f32[7,7,8,128]{3,2,1,0:T(8,128)S(1)}, f32[7,7,8,128]{3,2,1,0:T(8,128)S(1)}) %tuple.1216, (pred[]{:T(512)}, pred[]{:T(512)}, ...), branch_computations={%region_0.0_spmd, %region_1.0_spmd, %region_2.0_spmd, %region_3.0_... | conditional | flops 50176 | bytes 3010665 | solution.py:119
  48.9 3.5 %collective-permute-start.1 = (f32[7,7,8,128]{3,2,1,0:T(8,128)S(1)}, f32[7,7,8,128]{3,2,1,0:T(8,128)S(1)}, u32[]{:S(2)}, u32[]{:S(2)}) collective-permute-start(f32[7,7,8,128]{3,2,1,0:T(8,128)S(1)} %broadcast_select_fusion), channel_id=1, source_target_pairs={{0,124},{4,0},{8,4},{12,8},{16,12},{20,16},{24,20},{28,24},{32,28}... | collective-permute-start | bytes 602120 | tf_op jit(solution)/shard_map/cond/branch_0_fun/ppermute | solution.py:16
  52.4 3.9 %collective-permute-done.1 = f32[7,7,8,128]{3,2,1,0:T(8,128)S(1)} collective-permute-done((f32[7,7,8,128]{3,2,1,0:T(8,128)S(1)}, f32[7,7,8,128]{3,2,1,0:T(8,128)S(1)}, u32[]{:S(2)}, u32[]{:S(2)}) %collective-permute-start.1) | collective-permute-done | bytes 200736 | tf_op jit(solution)/shard_map/cond/branch_0_fun/ppermute | solution.py:16
  76.3 1.9 fusion.128
  78.2 10.7 %collective-permute-done.260 = f32[7,7,8,128]{3,1,2,0:T(8,128)S(1)} collective-permute-done((f32[7,7,8,128]{3,1,2,0:T(8,128)S(1)}, f32[7,7,8,128]{3,1,2,0:T(8,128)S(1)}, u32[]{:S(2)}, u32[]{:S(2)}) %collective-permute-start.260) | collective-permute-done | bytes 200736 | tf_op jit(solution)/shard_map/ppermute | solution.py:16
  101.8 1.8 fusion.18
  103.6 2.2 fusion.30
  106.8 3.7 %collective-permute-start.264 = (f32[1,7,7,8,128]{4,3,2,1,0:T(8,128)S(1)}, f32[1,7,7,8,128]{4,3,2,1,0:T(8,128)S(1)}, u32[]{:S(2)}, u32[]{:S(2)}) collective-permute-start(f32[1,7,7,8,128]{4,3,2,1,0:T(8,128)S(1)} %get-tuple-element.1830), channel_id=1, source_target_pairs={{1,0},{2,1},{3,2},{5,4},{6,5},{7,6},{9,8},{10,9},{11,10},{13,12},{... | collective-permute-start | bytes 602120 | tf_op jit(solution)/shard_map/ppermute | solution.py:29
  110.6 1.9 collective-permute-start.263
  113.4 7.2 %collective-permute-start.261 = (f32[2,7,7,8,1]{4,3,2,1,0:T(8,128)S(1)}, f32[2,7,7,8,1]{4,3,2,1,0:T(8,128)S(1)}, u32[]{:S(2)}, u32[]{:S(2)}) collective-permute-start(f32[2,7,7,8,1]{4,3,2,1,0:T(8,128)S(1)} %get-tuple-element.1847), channel_id=1, source_target_pairs={{4,0},{8,4},{12,8},{16,12},{20,16},{24,20},{28,24},{32,28},{36,32}... | collective-permute-start | bytes 9416 | tf_op jit(solution)/shard_map/ppermute | solution.py:29
  120.7 7.8 %collective-permute-done.261 = f32[2,7,7,8,1]{4,3,2,1,0:T(8,128)S(1)} collective-permute-done((f32[2,7,7,8,1]{4,3,2,1,0:T(8,128)S(1)}, f32[2,7,7,8,1]{4,3,2,1,0:T(8,128)S(1)}, u32[]{:S(2)}, u32[]{:S(2)}) %collective-permute-start.261) | collective-permute-done | bytes 3168 | tf_op jit(solution)/shard_map/ppermute | solution.py:29
  129.9 20.9 %conditional.5 = (pred[]{:T(512)}, f32[7,7,8,128]{3,1,2,0:T(8,128)S(1)}, f32[7,7,8,128]{3,1,2,0:T(8,128)S(1)}) conditional(s32[]{:T(128)} %clamp.13, (pred[]{:T(512)}, f32[7,7,8,128]{3,2,1,0:T(8,128)S(1)}, f32[7,7,8,128]{3,2,1,0:T(8,128)S(1)}) %tuple.1376, (pred[]{:T(512)}, f32[7,7,8,128]{3,2,1,0:T(8,128)S(1)}, ...), branch_computations={%region_33.34_spmd, %region_34.35_spmd, %region_35.36_spmd, %regio... | conditional | flops 50176 | bytes 3010665 | solution.py:119
  139.9 8.0 %collective-permute-start.126 = (f32[7,7,8,128]{3,2,1,0:T(8,128)S(1)}, f32[7,7,8,128]{3,2,1,0:T(8,128)S(1)}, u32[]{:S(2)}, u32[]{:S(2)}) collective-permute-start(f32[7,7,8,128]{3,2,1,0:T(8,128)S(1)} %broadcast_select_fusion.63), channel_id=1, source_target_pairs={{0,124},{4,0},{8,4},{12,8},{16,12},{20,16},{24,20},{28,24},{32,28}... | collective-permute-start | bytes 602120 | tf_op jit(solution)/shard_map/cond/branch_31_fun/ppermute | solution.py:16
  147.9 2.6 collective-permute-done.126
  150.9 1.8 fusion.118
  152.7 9.5 %collective-permute-done.265 = f32[7,7,8,128]{3,1,2,0:T(8,128)S(1)} collective-permute-done((f32[7,7,8,128]{3,1,2,0:T(8,128)S(1)}, f32[7,7,8,128]{3,1,2,0:T(8,128)S(1)}, u32[]{:S(2)}, u32[]{:S(2)}) %collective-permute-start.265) | collective-permute-done | bytes 200736 | tf_op jit(solution)/shard_map/ppermute | solution.py:16
  169.4 1.8 fusion.8
  171.2 1.8 fusion.20
  173.0 2.2 fusion.32
  176.3 5.3 %collective-permute-start.269 = (f32[1,7,7,8,128]{4,3,2,1,0:T(8,128)S(1)}, f32[1,7,7,8,128]{4,3,2,1,0:T(8,128)S(1)}, u32[]{:S(2)}, u32[]{:S(2)}) collective-permute-start(f32[1,7,7,8,128]{4,3,2,1,0:T(8,128)S(1)} %get-tuple-element.1826), channel_id=1, source_target_pairs={{1,0},{2,1},{3,2},{5,4},{6,5},{7,6},{9,8},{10,9},{11,10},{13,12},{... | collective-permute-start | bytes 602120 | tf_op jit(solution)/shard_map/ppermute | solution.py:29
  181.6 1.9 collective-permute-start.268
  184.5 7.2 %collective-permute-start.266 = (f32[2,7,7,8,1]{4,3,2,1,0:T(8,128)S(1)}, f32[2,7,7,8,1]{4,3,2,1,0:T(8,128)S(1)}, u32[]{:S(2)}, u32[]{:S(2)}) collective-permute-start(f32[2,7,7,8,1]{4,3,2,1,0:T(8,128)S(1)} %get-tuple-element.1845), channel_id=1, source_target_pairs={{4,0},{8,4},{12,8},{16,12},{20,16},{24,20},{28,24},{32,28},{36,32}... | collective-permute-start | bytes 9416 | tf_op jit(solution)/shard_map/ppermute | solution.py:29
  191.8 10.7 %collective-permute-done.266 = f32[2,7,7,8,1]{4,3,2,1,0:T(8,128)S(1)} collective-permute-done((f32[2,7,7,8,1]{4,3,2,1,0:T(8,128)S(1)}, f32[2,7,7,8,1]{4,3,2,1,0:T(8,128)S(1)}, u32[]{:S(2)}, u32[]{:S(2)}) %collective-permute-start.266) | collective-permute-done | bytes 3168 | tf_op jit(solution)/shard_map/ppermute | solution.py:29
  203.9 36.7 %conditional.6 = (pred[]{:T(512)}, f32[7,7,8,128]{3,1,2,0:T(8,128)S(1)}, f32[7,7,8,128]{3,1,2,0:T(8,128)S(1)}) conditional(s32[]{:T(128)} %clamp.14, (pred[]{:T(512)}, f32[7,7,8,128]{3,2,1,0:T(8,128)S(1)}, f32[7,7,8,128]{3,2,1,0:T(8,128)S(1)}) %tuple.1408, (pred[]{:T(512)}, f32[7,7,8,128]{3,2,1,0:T(8,128)S(1)}, ...), branch_computations={%region_66.67_spmd, %region_67.68_spmd, %region_68.69_spmd, %regio... | conditional | flops 50176 | bytes 3010665 | solution.py:119
  204.0 10.2 %collective-permute-start.144 = (f32[7,7,8,128]{3,2,1,0:T(8,128)S(1)}, f32[7,7,8,128]{3,2,1,0:T(8,128)S(1)}, u32[]{:S(2)}, u32[]{:S(2)}) collective-permute-start(f32[7,7,8,128]{3,2,1,0:T(8,128)S(1)} %broadcast_select_fusion.72), channel_id=1, source_target_pairs={{0,32},{4,36},{8,40},{12,44},{16,48},{20,52},{24,56},{28,60},{32,6... | collective-permute-start | bytes 602120 | tf_op jit(solution)/shard_map/cond/branch_8_fun/ppermute | solution.py:16
  214.2 2.1 collective-permute-done.145
  216.3 4.3 %collective-permute-done.144 = f32[7,7,8,128]{3,2,1,0:T(8,128)S(1)} collective-permute-done((f32[7,7,8,128]{3,2,1,0:T(8,128)S(1)}, f32[7,7,8,128]{3,2,1,0:T(8,128)S(1)}, u32[]{:S(2)}, u32[]{:S(2)}) %collective-permute-start.144) | collective-permute-done | bytes 200736 | tf_op jit(solution)/shard_map/cond/branch_8_fun/ppermute | solution.py:16
  240.7 1.8 fusion.108
  242.5 8.7 %collective-permute-done.270 = f32[7,7,8,128]{3,1,2,0:T(8,128)S(1)} collective-permute-done((f32[7,7,8,128]{3,1,2,0:T(8,128)S(1)}, f32[7,7,8,128]{3,1,2,0:T(8,128)S(1)}, u32[]{:S(2)}, u32[]{:S(2)}) %collective-permute-start.270) | collective-permute-done | bytes 200736 | tf_op jit(solution)/shard_map/ppermute | solution.py:16
  258.4 1.8 fusion.10
  260.2 1.8 fusion.22
  262.0 2.2 fusion.34
  265.2 6.9 %collective-permute-start.274 = (f32[1,7,7,8,128]{4,3,2,1,0:T(8,128)S(1)}, f32[1,7,7,8,128]{4,3,2,1,0:T(8,128)S(1)}, u32[]{:S(2)}, u32[]{:S(2)}) collective-permute-start(f32[1,7,7,8,128]{4,3,2,1,0:T(8,128)S(1)} %get-tuple-element.1820), channel_id=1, source_target_pairs={{1,0},{2,1},{3,2},{5,4},{6,5},{7,6},{9,8},{10,9},{11,10},{13,12},{... | collective-permute-start | bytes 602120 | tf_op jit(solution)/shard_map/ppermute | solution.py:29
  272.1 1.9 collective-permute-start.273
  275.0 7.2 %collective-permute-start.271 = (f32[2,7,7,8,1]{4,3,2,1,0:T(8,128)S(1)}, f32[2,7,7,8,1]{4,3,2,1,0:T(8,128)S(1)}, u32[]{:S(2)}, u32[]{:S(2)}) collective-permute-start(f32[2,7,7,8,1]{4,3,2,1,0:T(8,128)S(1)} %get-tuple-element.1843), channel_id=1, source_target_pairs={{4,0},{8,4},{12,8},{16,12},{20,16},{24,20},{28,24},{32,28},{36,32}... | collective-permute-start | bytes 9416 | tf_op jit(solution)/shard_map/ppermute | solution.py:29
  282.3 7.8 %collective-permute-done.271 = f32[2,7,7,8,1]{4,3,2,1,0:T(8,128)S(1)} collective-permute-done((f32[2,7,7,8,1]{4,3,2,1,0:T(8,128)S(1)}, f32[2,7,7,8,1]{4,3,2,1,0:T(8,128)S(1)}, u32[]{:S(2)}, u32[]{:S(2)}) %collective-permute-start.271) | collective-permute-done | bytes 3168 | tf_op jit(solution)/shard_map/ppermute | solution.py:29
  291.4 22.3 %conditional.7 = (pred[]{:T(512)}, f32[7,7,8,128]{3,1,2,0:T(8,128)S(1)}, f32[7,7,8,128]{3,1,2,0:T(8,128)S(1)}) conditional(s32[]{:T(128)} %clamp.15, (pred[]{:T(512)}, f32[7,7,8,128]{3,2,1,0:T(8,128)S(1)}, f32[7,7,8,128]{3,2,1,0:T(8,128)S(1)}) %tuple.1344, (pred[]{:T(512)}, f32[7,7,8,128]{3,2,1,0:T(8,128)S(1)}, ...), branch_computations={%region_99.100_spmd, %region_100.101_spmd, %region_101.102_spmd, %... | conditional | flops 50176 | bytes 3010665 | solution.py:119
  302.5 8.5 %collective-permute-start.250 = (f32[7,7,8,128]{3,2,1,0:T(8,128)S(1)}, f32[7,7,8,128]{3,2,1,0:T(8,128)S(1)}, u32[]{:S(2)}, u32[]{:S(2)}) collective-permute-start(f32[7,7,8,128]{3,2,1,0:T(8,128)S(1)} %broadcast_select_fusion.125), channel_id=1, source_target_pairs={{0,116},{4,120},{8,124},{12,0},{16,4},{20,8},{24,12},{28,16},{32,2... | collective-permute-start | bytes 602120 | tf_op jit(solution)/shard_map/cond/branch_29_fun/ppermute | solution.py:16
  311.0 2.4 collective-permute-done.251
  314.9 1.8 fusion.97
  316.8 7.6 %collective-permute-done.275 = f32[7,7,8,128]{3,1,2,0:T(8,128)S(1)} collective-permute-done((f32[7,7,8,128]{3,1,2,0:T(8,128)S(1)}, f32[7,7,8,128]{3,1,2,0:T(8,128)S(1)}, u32[]{:S(2)}, u32[]{:S(2)}) %collective-permute-start.275) | collective-permute-done | bytes 200736 | tf_op jit(solution)/shard_map/ppermute | solution.py:16
  (212 shorter events, 60.9 us)
Async XLA Ops:
  0.0 3.1 copy-start.11
  0.0 3.1 copy-start.30
  3.1 3.2 copy-start.24
  6.6 3.8 %copy-start.3 = (f32[1,1,7,7,7,8,128]{6,5,4,3,2,1,0:T(8,128)}, f32[1,1,7,7,7,8,128]{6,5,4,3,2,1,0:T(8,128)S(1)}, u32[]{:S(2)}) copy-start(f32[1,1,7,7,7,8,128]{6,5,4,3,2,1,0:T(8,128)S(1)} %get-tuple-element.1819) | copy-start | bytes 4214788
  6.6 97.0 %copy-start = (f32[1,1,7,7,7,8,128]{6,5,4,3,2,1,0:T(8,128)}, f32[1,1,7,7,7,8,128]{6,5,4,3,2,1,0:T(8,128)S(1)}, u32[]{:S(2)}) copy-start(f32[1,1,7,7,7,8,128]{6,5,4,3,2,1,0:T(8,128)S(1)} %get-tuple-element.1817) | copy-start | bytes 4214788
  12.8 17.8 %copy-start.32 = (s32[4]{0:T(128)S(1)}, s32[4]{0:T(128)}, u32[]{:S(2)}) copy-start(s32[4]{0:T(128)} %param.205) | copy-start | bytes 52
  12.9 25.7 %copy-start.33 = (f32[7]{0:T(128)S(1)}, f32[7]{0:T(128)}, u32[]{:S(2)}) copy-start(f32[7]{0:T(128)} %constant.707) | copy-start | bytes 88
  13.7 35.2 %collective-permute-start.259 = (f32[1,7,7,8,128]{4,3,2,1,0:T(8,128)}, f32[1,7,7,8,128]{4,3,2,1,0:T(8,128)S(1)}, u32[]{:S(2)}, u32[]{:S(2)}) collective-permute-start(f32[1,7,7,8,128]{4,3,2,1,0:T(8,128)} %get-tuple-element.1836), channel_id=1, source_target_pairs={{1,0},{2,1},{3,2},{5,4},{6,5},{7,6},{9,8},{10,9},{11,10},{13,12},{... | collective-permute-start | bytes 602120 | tf_op jit(solution)/shard_map/ppermute | solution.py:29
  16.9 31.9 %collective-permute-start.258 = (f32[1,7,7,8,128]{4,3,2,1,0:T(8,128)}, f32[1,7,7,8,128]{4,3,2,1,0:T(8,128)S(1)}, u32[]{:S(2)}, u32[]{:S(2)}) collective-permute-start(f32[1,7,7,8,128]{4,3,2,1,0:T(8,128)} %get-tuple-element.1837), channel_id=1, source_target_pairs={{0,1},{1,2},{2,3},{4,5},{5,6},{6,7},{8,9},{9,10},{10,11},{12,13},{... | collective-permute-start | bytes 602120 | tf_op jit(solution)/shard_map/ppermute | solution.py:26
  22.0 54.3 %collective-permute-start.257 = (f32[2,7,7,8,1]{4,3,2,1,0:T(8,128)}, f32[2,7,7,8,1]{4,3,2,1,0:T(8,128)}, u32[]{:S(2)}, u32[]{:S(2)}) collective-permute-start(f32[2,7,7,8,1]{4,3,2,1,0:T(8,128)} %get-tuple-element.1848), channel_id=1, source_target_pairs={{0,4},{4,8},{8,12},{12,16},{16,20},{20,24},{24,28},{28,32},{32,36}... | collective-permute-start | bytes 9416 | tf_op jit(solution)/shard_map/ppermute | solution.py:26
  23.7 20.8 %collective-permute-start.256 = (f32[2,7,7,8,1]{4,3,2,1,0:T(8,128)}, f32[2,7,7,8,1]{4,3,2,1,0:T(8,128)}, u32[]{:S(2)}, u32[]{:S(2)}) collective-permute-start(f32[2,7,7,8,1]{4,3,2,1,0:T(8,128)} %get-tuple-element.1849), channel_id=1, source_target_pairs={{4,0},{8,4},{12,8},{16,12},{20,16},{24,20},{28,24},{32,28},{36,32}... | collective-permute-start | bytes 9416 | tf_op jit(solution)/shard_map/ppermute | solution.py:29
  39.9 3.4 %copy-start.35 = (f32[7]{0:T(128)S(1)}, f32[7]{0:T(128)}, u32[]{:S(2)}) copy-start(f32[7]{0:T(128)} %constant.709) | copy-start | bytes 88
  39.9 3.5 %copy-start.34 = (pred[7,7]{1,0:T(8,128)(4,1)S(1)}, pred[7,7]{1,0:T(8,128)(4,1)}, u32[]{:S(2)}) copy-start(pred[7,7]{1,0:T(8,128)(4,1)} %constant.708) | copy-start | bytes 151
  39.9 4.0 %copy-start.31 = (f32[7]{0:T(128)S(1)}, f32[7]{0:T(128)}, u32[]{:S(2)}) copy-start(f32[7]{0:T(128)} %constant.702) | copy-start | bytes 88
  39.9 4.6 %copy-start.26 = (f32[1,7,7,8,128]{4,3,2,1,0:T(8,128)S(1)}, f32[1,7,7,8,128]{4,3,2,1,0:T(8,128)}, u32[]{:S(2)}) copy-start(f32[1,7,7,8,128]{4,3,2,1,0:T(8,128)} %copy-done.25) | copy-start | bytes 602116
  48.9 7.4 %collective-permute-start.1 = (f32[7,7,8,128]{3,2,1,0:T(8,128)S(1)}, f32[7,7,8,128]{3,2,1,0:T(8,128)S(1)}, u32[]{:S(2)}, u32[]{:S(2)}) collective-permute-start(f32[7,7,8,128]{3,2,1,0:T(8,128)S(1)} %broadcast_select_fusion), channel_id=1, source_target_pairs={{0,124},{4,0},{8,4},{12,8},{16,12},{20,16},{24,20},{28,24},{32,28}... | collective-permute-start | bytes 602120 | tf_op jit(solution)/shard_map/cond/branch_0_fun/ppermute | solution.py:16
  52.4 4.0 %collective-permute-start = (f32[7,7,8,128]{3,2,1,0:T(8,128)S(1)}, f32[7,7,8,128]{3,2,1,0:T(8,128)S(1)}, u32[]{:S(2)}, u32[]{:S(2)}) collective-permute-start(f32[7,7,8,128]{3,2,1,0:T(8,128)S(1)} %broadcast_select_fusion), channel_id=1, source_target_pairs={{0,0},{4,4},{8,8},{12,12},{16,16},{20,20},{24,24},{28,28},{32,32},... | collective-permute-start | bytes 602120 | tf_op jit(solution)/shard_map/cond/branch_0_fun/ppermute | solution.py:16
  76.2 12.7 %collective-permute-start.260 = (f32[7,7,8,128]{3,1,2,0:T(8,128)S(1)}, f32[7,7,8,128]{3,1,2,0:T(8,128)S(1)}, u32[]{:S(2)}, u32[]{:S(2)}) collective-permute-start(f32[7,7,8,128]{3,1,2,0:T(8,128)S(1)} %broadcast_select_fusion.131), channel_id=1, source_target_pairs={{0,4},{4,8},{8,12},{12,16},{16,20},{20,24},{24,28},{28,32},{32,36}... | collective-permute-start | bytes 602120 | tf_op jit(solution)/shard_map/ppermute | solution.py:16
  89.2 4.3 %copy-start.17 = (f32[1,7,7,7,8,128]{5,4,3,2,1,0:T(8,128)S(1)}, f32[1,7,7,7,8,128]{5,4,3,2,1,0:T(8,128)}, u32[]{:S(2)}) copy-start(f32[1,7,7,7,8,128]{5,4,3,2,1,0:T(8,128)} %param.204) | copy-start | bytes 4214788
  89.7 3.8 %copy-start.12 = (f32[1,7,7,7,8,128]{5,4,3,2,1,0:T(8,128)S(1)}, f32[1,7,7,7,8,128]{5,4,3,2,1,0:T(8,128)}, u32[]{:S(2)}) copy-start(f32[1,7,7,7,8,128]{5,4,3,2,1,0:T(8,128)} %param.201) | copy-start | bytes 4214788
  106.6 22.1 %copy-start.27 = (f32[1,7,7,8,128]{4,3,2,1,0:T(8,128)}, f32[1,7,7,8,128]{4,3,2,1,0:T(8,128)S(1)}, u32[]{:S(2)}) copy-start(f32[1,7,7,8,128]{4,3,2,1,0:T(8,128)S(1)} %get-tuple-element.1833) | copy-start | bytes 602116
  106.8 23.1 %collective-permute-start.264 = (f32[1,7,7,8,128]{4,3,2,1,0:T(8,128)S(1)}, f32[1,7,7,8,128]{4,3,2,1,0:T(8,128)S(1)}, u32[]{:S(2)}, u32[]{:S(2)}) collective-permute-start(f32[1,7,7,8,128]{4,3,2,1,0:T(8,128)S(1)} %get-tuple-element.1830), channel_id=1, source_target_pairs={{1,0},{2,1},{3,2},{5,4},{6,5},{7,6},{9,8},{10,9},{11,10},{13,12},{... | collective-permute-start | bytes 602120 | tf_op jit(solution)/shard_map/ppermute | solution.py:29
  110.6 19.3 %collective-permute-start.263 = (f32[1,7,7,8,128]{4,3,2,1,0:T(8,128)S(1)}, f32[1,7,7,8,128]{4,3,2,1,0:T(8,128)S(1)}, u32[]{:S(2)}, u32[]{:S(2)}) collective-permute-start(f32[1,7,7,8,128]{4,3,2,1,0:T(8,128)S(1)} %get-tuple-element.1831), channel_id=1, source_target_pairs={{0,1},{1,2},{2,3},{4,5},{5,6},{6,7},{8,9},{9,10},{10,11},{12,13},{... | collective-permute-start | bytes 602120 | tf_op jit(solution)/shard_map/ppermute | solution.py:26
  113.4 37.5 %collective-permute-start.262 = (f32[2,7,7,8,1]{4,3,2,1,0:T(8,128)}, f32[2,7,7,8,1]{4,3,2,1,0:T(8,128)}, u32[]{:S(2)}, u32[]{:S(2)}) collective-permute-start(f32[2,7,7,8,1]{4,3,2,1,0:T(8,128)} %get-tuple-element.1846), channel_id=1, source_target_pairs={{0,4},{4,8},{8,12},{12,16},{16,20},{20,24},{24,28},{28,32},{32,36}... | collective-permute-start | bytes 9416 | tf_op jit(solution)/shard_map/ppermute | solution.py:26
  113.4 15.0 %collective-permute-start.261 = (f32[2,7,7,8,1]{4,3,2,1,0:T(8,128)S(1)}, f32[2,7,7,8,1]{4,3,2,1,0:T(8,128)S(1)}, u32[]{:S(2)}, u32[]{:S(2)}) collective-permute-start(f32[2,7,7,8,1]{4,3,2,1,0:T(8,128)S(1)} %get-tuple-element.1847), channel_id=1, source_target_pairs={{4,0},{8,4},{12,8},{16,12},{20,16},{24,20},{28,24},{32,28},{36,32}... | collective-permute-start | bytes 9416 | tf_op jit(solution)/shard_map/ppermute | solution.py:29
  139.9 8.0 %collective-permute-start.127 = (f32[7,7,8,128]{3,2,1,0:T(8,128)S(1)}, f32[7,7,8,128]{3,2,1,0:T(8,128)S(1)}, u32[]{:S(2)}, u32[]{:S(2)}) collective-permute-start(f32[7,7,8,128]{3,2,1,0:T(8,128)S(1)} %broadcast_select_fusion.63), channel_id=1, source_target_pairs={{0,0},{4,4},{8,8},{12,12},{16,16},{20,20},{24,24},{28,28},{32,32},... | collective-permute-start | bytes 602120 | tf_op jit(solution)/shard_map/cond/branch_31_fun/ppermute | solution.py:16
  139.9 10.7 %collective-permute-start.126 = (f32[7,7,8,128]{3,2,1,0:T(8,128)S(1)}, f32[7,7,8,128]{3,2,1,0:T(8,128)S(1)}, u32[]{:S(2)}, u32[]{:S(2)}) collective-permute-start(f32[7,7,8,128]{3,2,1,0:T(8,128)S(1)} %broadcast_select_fusion.63), channel_id=1, source_target_pairs={{0,124},{4,0},{8,4},{12,8},{16,12},{20,16},{24,20},{28,24},{32,28}... | collective-permute-start | bytes 602120 | tf_op jit(solution)/shard_map/cond/branch_31_fun/ppermute | solution.py:16
  150.8 11.4 %collective-permute-start.265 = (f32[7,7,8,128]{3,1,2,0:T(8,128)S(1)}, f32[7,7,8,128]{3,1,2,0:T(8,128)S(1)}, u32[]{:S(2)}, u32[]{:S(2)}) collective-permute-start(f32[7,7,8,128]{3,1,2,0:T(8,128)S(1)} %broadcast_select_fusion.130), channel_id=1, source_target_pairs={{0,4},{4,8},{8,12},{12,16},{16,20},{20,24},{24,28},{28,32},{32,36}... | collective-permute-start | bytes 602120 | tf_op jit(solution)/shard_map/ppermute | solution.py:16
  152.7 10.7 %copy-start.21 = (f32[7,7,7,8,128]{4,3,2,1,0:T(8,128)S(1)}, f32[7,7,7,8,128]{4,3,2,1,0:T(8,128)}, u32[]{:S(2)}) copy-start(f32[7,7,7,8,128]{4,3,2,1,0:T(8,128)} %fusion.118) | copy-start | bytes 4214788
  173.0 2.3 copy-start.15
  176.1 26.4 %copy-start.29 = (f32[1,7,7,8,128]{4,3,2,1,0:T(8,128)}, f32[1,7,7,8,128]{4,3,2,1,0:T(8,128)S(1)}, u32[]{:S(2)}) copy-start(f32[1,7,7,8,128]{4,3,2,1,0:T(8,128)S(1)} %slice_bitcast_fusion.3) | copy-start | bytes 602116
  176.3 27.5 %collective-permute-start.269 = (f32[1,7,7,8,128]{4,3,2,1,0:T(8,128)S(1)}, f32[1,7,7,8,128]{4,3,2,1,0:T(8,128)S(1)}, u32[]{:S(2)}, u32[]{:S(2)}) collective-permute-start(f32[1,7,7,8,128]{4,3,2,1,0:T(8,128)S(1)} %get-tuple-element.1826), channel_id=1, source_target_pairs={{1,0},{2,1},{3,2},{5,4},{6,5},{7,6},{9,8},{10,9},{11,10},{13,12},{... | collective-permute-start | bytes 602120 | tf_op jit(solution)/shard_map/ppermute | solution.py:29
  181.6 22.2 %collective-permute-start.268 = (f32[1,7,7,8,128]{4,3,2,1,0:T(8,128)S(1)}, f32[1,7,7,8,128]{4,3,2,1,0:T(8,128)S(1)}, u32[]{:S(2)}, u32[]{:S(2)}) collective-permute-start(f32[1,7,7,8,128]{4,3,2,1,0:T(8,128)S(1)} %get-tuple-element.1827), channel_id=1, source_target_pairs={{0,1},{1,2},{2,3},{4,5},{5,6},{6,7},{8,9},{9,10},{10,11},{12,13},{... | collective-permute-start | bytes 602120 | tf_op jit(solution)/shard_map/ppermute | solution.py:26
  184.5 56.2 %collective-permute-start.267 = (f32[2,7,7,8,1]{4,3,2,1,0:T(8,128)}, f32[2,7,7,8,1]{4,3,2,1,0:T(8,128)}, u32[]{:S(2)}, u32[]{:S(2)}) collective-permute-start(f32[2,7,7,8,1]{4,3,2,1,0:T(8,128)} %get-tuple-element.1844), channel_id=1, source_target_pairs={{0,4},{4,8},{8,12},{12,16},{16,20},{20,24},{24,28},{28,32},{32,36}... | collective-permute-start | bytes 9416 | tf_op jit(solution)/shard_map/ppermute | solution.py:26
  184.5 18.0 %collective-permute-start.266 = (f32[2,7,7,8,1]{4,3,2,1,0:T(8,128)S(1)}, f32[2,7,7,8,1]{4,3,2,1,0:T(8,128)S(1)}, u32[]{:S(2)}, u32[]{:S(2)}) collective-permute-start(f32[2,7,7,8,1]{4,3,2,1,0:T(8,128)S(1)} %get-tuple-element.1845), channel_id=1, source_target_pairs={{4,0},{8,4},{12,8},{16,12},{20,16},{24,20},{28,24},{32,28},{36,32}... | collective-permute-start | bytes 9416 | tf_op jit(solution)/shard_map/ppermute | solution.py:29
  203.9 12.4 %collective-permute-start.145 = (f32[7,7,8,128]{3,2,1,0:T(8,128)S(1)}, f32[7,7,8,128]{3,2,1,0:T(8,128)S(1)}, u32[]{:S(2)}, u32[]{:S(2)}) collective-permute-start(f32[7,7,8,128]{3,2,1,0:T(8,128)S(1)} %broadcast_select_fusion.72), channel_id=1, source_target_pairs={{0,92},{4,96},{8,100},{12,104},{16,108},{20,112},{24,116},{28,120}... | collective-permute-start | bytes 602120 | tf_op jit(solution)/shard_map/cond/branch_8_fun/ppermute | solution.py:16
  204.0 16.6 %collective-permute-start.144 = (f32[7,7,8,128]{3,2,1,0:T(8,128)S(1)}, f32[7,7,8,128]{3,2,1,0:T(8,128)S(1)}, u32[]{:S(2)}, u32[]{:S(2)}) collective-permute-start(f32[7,7,8,128]{3,2,1,0:T(8,128)S(1)} %broadcast_select_fusion.72), channel_id=1, source_target_pairs={{0,32},{4,36},{8,40},{12,44},{16,48},{20,52},{24,56},{28,60},{32,6... | collective-permute-start | bytes 602120 | tf_op jit(solution)/shard_map/cond/branch_8_fun/ppermute | solution.py:16
  240.6 10.7 %collective-permute-start.270 = (f32[7,7,8,128]{3,1,2,0:T(8,128)S(1)}, f32[7,7,8,128]{3,1,2,0:T(8,128)S(1)}, u32[]{:S(2)}, u32[]{:S(2)}) collective-permute-start(f32[7,7,8,128]{3,1,2,0:T(8,128)S(1)} %broadcast_select_fusion.129), channel_id=1, source_target_pairs={{0,4},{4,8},{8,12},{12,16},{16,20},{20,24},{24,28},{28,32},{32,36}... | collective-permute-start | bytes 602120 | tf_op jit(solution)/shard_map/ppermute | solution.py:16
  242.5 9.9 %copy-start.22 = (f32[7,7,7,8,128]{4,3,2,1,0:T(8,128)S(1)}, f32[7,7,7,8,128]{4,3,2,1,0:T(8,128)}, u32[]{:S(2)}) copy-start(f32[7,7,7,8,128]{4,3,2,1,0:T(8,128)} %fusion.108) | copy-start | bytes 4214788
  265.0 25.0 %copy-start.28 = (f32[1,7,7,8,128]{4,3,2,1,0:T(8,128)}, f32[1,7,7,8,128]{4,3,2,1,0:T(8,128)S(1)}, u32[]{:S(2)}) copy-start(f32[1,7,7,8,128]{4,3,2,1,0:T(8,128)S(1)} %get-tuple-element.1823) | copy-start | bytes 602116
  265.2 26.2 %collective-permute-start.274 = (f32[1,7,7,8,128]{4,3,2,1,0:T(8,128)S(1)}, f32[1,7,7,8,128]{4,3,2,1,0:T(8,128)S(1)}, u32[]{:S(2)}, u32[]{:S(2)}) collective-permute-start(f32[1,7,7,8,128]{4,3,2,1,0:T(8,128)S(1)} %get-tuple-element.1820), channel_id=1, source_target_pairs={{1,0},{2,1},{3,2},{5,4},{6,5},{7,6},{9,8},{10,9},{11,10},{13,12},{... | collective-permute-start | bytes 602120 | tf_op jit(solution)/shard_map/ppermute | solution.py:29
  272.1 19.3 %collective-permute-start.273 = (f32[1,7,7,8,128]{4,3,2,1,0:T(8,128)S(1)}, f32[1,7,7,8,128]{4,3,2,1,0:T(8,128)S(1)}, u32[]{:S(2)}, u32[]{:S(2)}) collective-permute-start(f32[1,7,7,8,128]{4,3,2,1,0:T(8,128)S(1)} %get-tuple-element.1821), channel_id=1, source_target_pairs={{0,1},{1,2},{2,3},{4,5},{5,6},{6,7},{8,9},{9,10},{10,11},{12,13},{... | collective-permute-start | bytes 602120 | tf_op jit(solution)/shard_map/ppermute | solution.py:26
  275.0 40.0 %collective-permute-start.272 = (f32[2,7,7,8,1]{4,3,2,1,0:T(8,128)}, f32[2,7,7,8,1]{4,3,2,1,0:T(8,128)}, u32[]{:S(2)}, u32[]{:S(2)}) collective-permute-start(f32[2,7,7,8,1]{4,3,2,1,0:T(8,128)} %get-tuple-element.1842), channel_id=1, source_target_pairs={{0,4},{4,8},{8,12},{12,16},{16,20},{20,24},{24,28},{28,32},{32,36}... | collective-permute-start | bytes 9416 | tf_op jit(solution)/shard_map/ppermute | solution.py:26
  275.0 15.0 %collective-permute-start.271 = (f32[2,7,7,8,1]{4,3,2,1,0:T(8,128)S(1)}, f32[2,7,7,8,1]{4,3,2,1,0:T(8,128)S(1)}, u32[]{:S(2)}, u32[]{:S(2)}) collective-permute-start(f32[2,7,7,8,1]{4,3,2,1,0:T(8,128)S(1)} %get-tuple-element.1843), channel_id=1, source_target_pairs={{4,0},{8,4},{12,8},{16,12},{20,16},{24,20},{28,24},{32,28},{36,32}... | collective-permute-start | bytes 9416 | tf_op jit(solution)/shard_map/ppermute | solution.py:29
  302.4 11.0 %collective-permute-start.251 = (f32[7,7,8,128]{3,2,1,0:T(8,128)S(1)}, f32[7,7,8,128]{3,2,1,0:T(8,128)S(1)}, u32[]{:S(2)}, u32[]{:S(2)}) collective-permute-start(f32[7,7,8,128]{3,2,1,0:T(8,128)S(1)} %broadcast_select_fusion.125), channel_id=1, source_target_pairs={{0,8},{4,12},{8,16},{12,20},{16,24},{20,28},{24,32},{28,36},{32,40... | collective-permute-start | bytes 602120 | tf_op jit(solution)/shard_map/cond/branch_29_fun/ppermute | solution.py:16
  302.5 11.1 %collective-permute-start.250 = (f32[7,7,8,128]{3,2,1,0:T(8,128)S(1)}, f32[7,7,8,128]{3,2,1,0:T(8,128)S(1)}, u32[]{:S(2)}, u32[]{:S(2)}) collective-permute-start(f32[7,7,8,128]{3,2,1,0:T(8,128)S(1)} %broadcast_select_fusion.125), channel_id=1, source_target_pairs={{0,116},{4,120},{8,124},{12,0},{16,4},{20,8},{24,12},{28,16},{32,2... | collective-permute-start | bytes 602120 | tf_op jit(solution)/shard_map/cond/branch_29_fun/ppermute | solution.py:16
  313.7 10.7 %collective-permute-start.275 = (f32[7,7,8,128]{3,1,2,0:T(8,128)S(1)}, f32[7,7,8,128]{3,1,2,0:T(8,128)S(1)}, u32[]{:S(2)}, u32[]{:S(2)}) collective-permute-start(f32[7,7,8,128]{3,1,2,0:T(8,128)S(1)} %broadcast_select_fusion.128), channel_id=1, source_target_pairs={{0,4},{4,8},{8,12},{12,16},{16,20},{20,24},{24,28},{28,32},{32,36}... | collective-permute-start | bytes 602120 | tf_op jit(solution)/shard_map/ppermute | solution.py:16
  316.8 8.8 %copy-start.23 = (f32[7,7,7,8,128]{4,3,2,1,0:T(8,128)S(1)}, f32[7,7,7,8,128]{4,3,2,1,0:T(8,128)}, u32[]{:S(2)}) copy-start(f32[7,7,7,8,128]{4,3,2,1,0:T(8,128)} %fusion.97) | copy-start | bytes 4214788
  (16 other events, 26.6 us)
where the time goes:
time: 333 us; the launch traced here: 328 us
  starting transfers between devices  90.1 us (27%)
  waiting for transfers between devices  78.5 us (24%)
  loops' own time  60.8 us (18%)
  matrix products  46.7 us (14%)
  other arithmetic  30.1 us (9%)
  local copies, waits for them, and re-layouts  13 us (4%)
  between operations  9.08 us (3%)
    another operation x4, loops' own time, rotate_window(): rotated = lax.switch(sector_k, branches, block)  60.8 us
    ppermute x12, waiting for transfers between devices, passed_along(): return lax.ppermute(value, axis, pairs)  52.2 us
    ppermute x8, starting transfers between devices, padded_2(): lax.ppermute(lax.slice_in_dim(block, 0, width, axis=dim), axis, backward)  47.7 us
    ppermute x12, starting transfers between devices, passed_along(): return lax.ppermute(value, axis, pairs)  31.7 us
    ppermute x8, waiting for transfers between devices, padded_2(): lax.ppermute(lax.slice_in_dim(block, 0, width, axis=dim), axis, backward)  26.2 us
    ppermute x8, starting transfers between devices, padded_2(): lax.ppermute(lax.slice_in_dim(block, block.shape[dim] - width, None, axis...  10.7 us
    dot_general x4, matrix products, element_apply(): jnp.einsum('pa,prcxe->arcxe', derivative, coeffs[0] * grad_axial, precisi...  8.61 us
    dot_general x4, matrix products, element_apply(): jnp.einsum('pr,arcxe->apcxe', derivative, field, precision=highest)  7.92 us
  transfers between devices with their start and end apart: 28, of which 13 were waited for; matrix products, arithmetic and copies ran while one was open for 8% of the time, Pallas kernels for 0%

commit v1 on v0

v1 whole, which is shorter than its diff:
```python
import jax
import jax.numpy as jnp
import numpy as np
from jax import lax
from jax.experimental import pallas as pl
from jax.experimental.pallas import tpu as pltpu
from jax.sharding import PartitionSpec as P

SUBSTEPS = 3
STEPS = 4
N = 7
NY = 4
NZ = 4
MESH = pl.DeviceIdType.MESH


def gll_points():
    return np.array(
        [-1.0, -0.830223896278567, -0.4688487934707142, 0.0,
         0.4688487934707142, 0.830223896278567, 1.0]
    )


def derivative_table():
    points = gll_points()
    weights = np.array(
        [1.0 / np.prod([points[j] - points[k] for k in range(N) if k != j]) for j in range(N)]
    )
    derivative = np.zeros((N, N))
    for i in range(N):
        for j in range(N):
            if i != j:
                derivative[i, j] = weights[j] / weights[i] / (points[i] - points[j])
        derivative[i, i] = -np.sum(derivative[i])
    return derivative


def lagrange_row(location):
    points = gll_points()
    return np.array(
        [np.prod([(location - points[q]) / (points[n] - points[q]) for q in range(N) if q != n])
         for n in range(N)]
    )


def mortar_constants():
    heights = (1.0 + gll_points()) * 0.5
    table = np.zeros((2, SUBSTEPS, 2, N, N))
    for residue in range(SUBSTEPS):
        fraction = residue / SUBSTEPS
        rows = []
        for m in range(N):
            local = heights[m] - fraction
            if heights[m] < fraction:
                local += 1.0
            rows.append(lagrange_row(2.0 * local - 1.0))
        both = np.array(rows)
        table[0, residue, 0] = both
        table[0, residue, 1] = both.T
        table[1, residue, 0] = np.eye(N)
        table[1, residue, 1] = np.eye(N)
    return table.astype(np.float32)


def left_counts():
    heights = (1.0 + gll_points()) * 0.5
    return [int(np.sum(heights < residue / SUBSTEPS)) for residue in range(SUBSTEPS)]


DERIV = derivative_table()
LEFT = left_counts()


def half_line(matrix, v):
    even = [v[q] + v[6 - q] for q in range(3)]
    odd = [v[q] - v[6 - q] for q in range(3)]
    out = [None] * N
    for p in range(3):
        e = float(matrix[p, 3]) * v[3]
        o = None
        for q in range(3):
            e = e + float(0.5 * (matrix[p, q] + matrix[p, 6 - q])) * even[q]
            term = float(0.5 * (matrix[p, q] - matrix[p, 6 - q])) * odd[q]
            o = term if o is None else o + term
        out[p] = o + e
        out[6 - p] = o - e
    out[3] = (
        float(matrix[3, 0]) * odd[0] + float(matrix[3, 1]) * odd[1] + float(matrix[3, 2]) * odd[2]
    )
    return out


def apply_line(v, coeff):
    grad = half_line(DERIV, v)
    return half_line(DERIV.T, [coeff[p] * grad[p] for p in range(N)])


def kernel(
    rot, table, field, coeffs, reaction, scale, out,
    u, co, re, sc, ap, splat, codes, face, delta, diag,
    halo_src, halo_dst, side_dst,
    zsrc, zdst, ysrc, ydst, xsrc, xdst,
    load_u, load_c, load_s, store_sem,
    halo_send, halo_recv, side_send, side_recv,
    zsend, zrecv, ysend, yrecv, xsend, xrecv,
):
    c = lax.axis_index("circ")
    side = lax.axis_index("side")
    count = lax.axis_size("circ")
    z_me = c % NZ
    y_me = (c // NZ) % NY
    x_me = c // (NZ * NY)
    is_mortar = (side == 1) | (side == 2)
    is_rotor = side < 2
    parity = side % 2
    partner = side + 1 - 2 * parity
    fp = 6 - 6 * parity
    fm = 6 * parity
    lane = lax.broadcasted_iota(jnp.int32, (8, 128), 1)
    row = lax.broadcasted_iota(jnp.int32, (8, 128), 0)

    def at(xx, yy, zz):
        return (xx * NY + yy) * NZ + zz

    nxt = (c + 1) % count
    prv = (c + count - 1) % count
    z_dev = [at(x_me, y_me, (z_me + j + 1) % NZ) for j in range(3)]
    y_dev = [at(x_me, (y_me + j + 1) % NY, z_me) for j in range(3)]
    x_dev = [at((x_me + j) % 2, y_me, z_me) for j in range(2)]
    across = 3 - side

    def load_slice(a):
        return [
            pltpu.make_async_copy(field.at[a], u.at[a], load_u.at[a, 0]),
            pltpu.make_async_copy(reaction.at[a], re.at[a], load_u.at[a, 1]),
            pltpu.make_async_copy(coeffs.at[1, a], co.at[1, a], load_u.at[a, 2]),
            pltpu.make_async_copy(coeffs.at[2, a], co.at[2, a], load_u.at[a, 3]),
        ]

    load_axial = pltpu.make_async_copy(coeffs.at[0], co.at[0], load_c)
    load_scale = pltpu.make_async_copy(scale, sc, load_s)

    barrier = pltpu.get_barrier_semaphore()

    def greet(cc, ss):
        pl.semaphore_signal(
            barrier, inc=1, device_id={"circ": cc, "side": ss}, device_id_type=MESH
        )

    greet(nxt, side)
    greet(prv, side)
    greet(c, partner)

    @pl.when(is_mortar)
    def _():
        for d in z_dev + y_dev:
            greet(d, side)
        for d in x_dev:
            greet(d, across)

    def issue(a, carry):
        for copy in load_slice(a):
            copy.start()
        return carry

    lax.fori_loop(0, N, issue, 0)
    load_axial.start()
    load_scale.start()

    def digits(shift):
        s = shift & 127
        total = ((shift >> 7) + jnp.where(lane < s, 1, 0)) & 31
        dz = total & 3
        dy = ((total >> 2) & 3) + jnp.where(z_me < dz, 1, 0)
        dx = ((total >> 4) + jnp.where(y_me < dy, 1, 0)) & 1
        return dz, dy & 3, dx

    @pl.when(is_mortar)
    def _():
        def prepare(t, carry):
            offset = rot[t]
            k = offset // SUBSTEPS
            residue = offset - k * SUBSTEPS
            left = jnp.where(residue == 0, LEFT[0], jnp.where(residue == 1, LEFT[1], LEFT[2]))
            cycle = count * 128
            for m in range(N):
                kappa = k + jnp.where(m < left, 1, 0)
                kappa = jnp.where(kappa >= cycle, kappa - cycle, kappa)
                back = jnp.where(kappa == 0, 0, cycle - kappa)
                dz, dy, _ = digits(jnp.where(is_rotor, kappa, back))
                codes[t, 0, m] = dz
                codes[t, 1, m] = dy
                codes[t, 2, m] = digits(jnp.where(is_rotor, back, kappa))[2]
            half = jnp.where(is_rotor, 0, 1)
            first = (half * SUBSTEPS + residue) * 2 * N * N
            for i in range(2 * N * N):
                splat[t, i] = jnp.full((8, 128), table[first + i], jnp.float32)
            return carry

        lax.fori_loop(0, STEPS, prepare, 0)

    def in_face(a):
        for cc in range(N):
            line = [u[a, r, cc] for r in range(N)]
            res = apply_line(line, [co[1, a, p, cc] for p in range(N)])
            for r in range(N):
                ap[a, r, cc] = res[r] + re[a, r, cc] * line[r]
        for r in range(N):
            line = [u[a, r, cc] for cc in range(N)]
            res = apply_line(line, [co[2, a, r, p] for p in range(N)])
            for cc in range(N):
                ap[a, r, cc] = ap[a, r, cc] + res[cc]

    def axial(r, carry):
        for cc in range(N):
            line = [u[a, r, cc] for a in range(N)]
            res = apply_line(line, [co[0, p, r, cc] for p in range(N)])
            for a in range(N):
                ap[a, r, cc] = ap[a, r, cc] + res[a]
        return carry

    def first_slice(a, carry):
        for copy in load_slice(a):
            copy.wait()
        in_face(a)
        return carry

    def next_slice(a, carry):
        in_face(a)
        return carry

    lax.fori_loop(0, N, first_slice, 0)
    load_axial.wait()
    lax.fori_loop(0, N, axial, 0)
    load_scale.wait()

    edge = [jnp.where(parity == 1, float(DERIV[p, 6]), float(DERIV[p, 0])) for p in range(N)]

    @pl.when(is_mortar)
    def _():
        def body(r, carry):
            for cc in range(N):
                total = re[fm, r, cc]
                for p in range(N):
                    total = total + float(DERIV[p, 0]) ** 2 * jnp.where(
                        parity == 1, co[0, 6 - p, r, cc], co[0, p, r, cc]
                    )
                diag[r, cc] = total
                face[r, cc] = ap[fm, r, cc]
            return carry

        lax.fori_loop(0, N, body, 0)

    @pl.when(is_mortar)
    def _():
        pl.semaphore_wait(barrier, 11)

    @pl.when(jnp.logical_not(is_mortar))
    def _():
        pl.semaphore_wait(barrier, 3)

    def hop(src, dst, send, recv, cc, ss):
        return pltpu.make_async_remote_copy(
            src_ref=src, dst_ref=dst, send_sem=send, recv_sem=recv,
            device_id={"circ": cc, "side": ss}, device_id_type=MESH,
        )

    def z_hop(t, r, j):
        return hop(zsrc.at[t, r], zdst.at[t, j, r], zsend.at[t, j, r], zrecv.at[t, j, r], z_dev[j], side)

    def y_hop(t, r, j):
        return hop(ysrc.at[t, r], ydst.at[t, j, r], ysend.at[t, j, r], yrecv.at[t, j, r], y_dev[j], side)

    def x_hop(t, r, j):
        return hop(xsrc.at[t, r], xdst.at[t, j, r], xsend.at[t, j, r], xrecv.at[t, j, r], x_dev[j], across)

    def step(t, carry):
        @pl.when(is_mortar)
        def _():
            offset = rot[t]
            k = offset // SUBSTEPS
            residue = offset - k * SUBSTEPS
            left = jnp.where(residue == 0, LEFT[0], jnp.where(residue == 1, LEFT[1], LEFT[2]))
            shifts = []
            for m in range(N):
                kappa = k + jnp.where(m < left, 1, 0)
                shifts.append(jnp.where(is_rotor, kappa, 128 * 64 - kappa) & 127)

            def send(r, carry):
                nodes = [face[r, n] for n in range(N)]
                for m in range(N):
                    total = splat[t, m * N] * nodes[0]
                    for n in range(1, N):
                        total = total + splat[t, m * N + n] * nodes[n]
                    zsrc[t, r, m] = pltpu.roll(total, shifts[m], 1)
                for j in range(3):
                    z_hop(t, r, j).start()
                return carry

            lax.fori_loop(0, N, send, 0)

            @pl.when(t > 0)
            def _():
                def rest(r, carry):
                    for cc in range(N):
                        d = delta[r, cc]
                        res = half_line(DERIV.T, [(edge[p] * d) * co[0, p, r, cc] for p in range(N)])
                        for a in range(N):
                            ap[a, r, cc] = ap[a, r, cc] + res[a]
                    for cc in range(N):
                        ap[fm, r, cc] = face[r, cc]
                    return carry

                lax.fori_loop(0, N, rest, 0)

        side_copy = hop(ap.at[fp], side_dst.at[t], side_send.at[t], side_recv.at[t], c, partner)
        side_copy.start()

        def pack(a, carry):
            low, high = carry
            for r in range(N):
                here = lane == a * N + r
                low = jnp.where(here, jnp.broadcast_to(ap[a, r, 0][:, 0:1], (8, 128)), low)
                high = jnp.where(here, jnp.broadcast_to(ap[a, r, 6][:, 127:128], (8, 128)), high)
            return low, high

        zero = jnp.zeros((8, 128), jnp.float32)
        low, high = lax.fori_loop(0, N, pack, (zero, zero))
        halo_src[t, 0] = low
        halo_src[t, 1] = high
        low_copy = hop(halo_src.at[t, 0], halo_dst.at[t, 0], halo_send.at[t, 0], halo_recv.at[t, 0], prv, side)
        high_copy = hop(halo_src.at[t, 1], halo_dst.at[t, 1], halo_send.at[t, 1], halo_recv.at[t, 1], nxt, side)
        low_copy.start()
        high_copy.start()
        low_copy.wait()
        high_copy.wait()

        def advance(a, carry):
            after, before = carry
            for r in range(N):
                for cc in range(N):
                    total = ap[a, r, cc]
                    if r == 6:
                        total = total + jnp.where(row == 7, 0.0, pltpu.roll(ap[a, 0, cc], 7, 0))
                    if r == 0:
                        total = total + jnp.where(row == 0, 0.0, pltpu.roll(ap[a, 6, cc], 1, 0))
                    if cc == 6:
                        other = jnp.broadcast_to(after[:, r:r + 1], (8, 128))
                        total = total + jnp.where(lane == 127, other, pltpu.roll(ap[a, r, 0], 127, 1))
                    if cc == 0:
                        other = jnp.broadcast_to(before[:, r:r + 1], (8, 128))
                        total = total + jnp.where(lane == 0, other, pltpu.roll(ap[a, r, 6], 1, 1))
                    u[a, r, cc] = u[a, r, cc] - sc[a, r, cc] * total
            return pltpu.roll(after, 128 - N, 1), pltpu.roll(before, 128 - N, 1)

        lax.fori_loop(0, N, advance, (halo_dst[t, 0], halo_dst[t, 1]))
        side_copy.wait()

        def add_side(r, carry):
            for cc in range(N):
                u[fp, r, cc] = u[fp, r, cc] - sc[fp, r, cc] * side_dst[t, r, cc]
            return carry

        lax.fori_loop(0, N, add_side, 0)

        @pl.when(is_mortar)
        def _():
            def along_y(r, carry):
                for j in range(3):
                    z_hop(t, r, j).wait_recv()
                for m in range(N):
                    code = codes[t, 0, m]
                    low = jnp.where(code == 0, zsrc[t, r, m], zdst[t, 0, r, m])
                    high = jnp.where(code == 2, zdst[t, 1, r, m], zdst[t, 2, r, m])
                    ysrc[t, r, m] = jnp.where(code < 2, low, high)
                for j in range(3):
                    y_hop(t, r, j).start()
                return carry

            lax.fori_loop(0, N, along_y, 0)

            def along_x(r, carry):
                for j in range(3):
                    y_hop(t, r, j).wait_recv()
                for m in range(N):
                    code = codes[t, 1, m]
                    low = jnp.where(code == 0, ysrc[t, r, m], ydst[t, 0, r, m])
                    high = jnp.where(code == 2, ydst[t, 1, r, m], ydst[t, 2, r, m])
                    xsrc[t, r, m] = jnp.where(code < 2, low, high)
                for j in range(2):
                    x_hop(t, r, j).start()
                return carry

            lax.fori_loop(0, N, along_x, 0)

        @pl.when(t < STEPS - 1)
        def _():
            lax.fori_loop(0, N, next_slice, 0)
            lax.fori_loop(0, N, axial, 0)

        @pl.when(is_mortar)
        def _():
            def arrive(r, carry):
                for j in range(2):
                    x_hop(t, r, j).wait_recv()
                nodes = [
                    jnp.where(codes[t, 2, m] == 0, xdst[t, 0, r, m], xdst[t, 1, r, m])
                    for m in range(N)
                ]
                for n in range(N):
                    total = splat[t, N * N + n * N] * nodes[0]
                    for m in range(1, N):
                        total = total + splat[t, N * N + n * N + m] * nodes[m]
                    change = -(sc[fm, r, n] * total)
                    delta[r, n] = change
                    u[fm, r, n] = u[fm, r, n] + change
                return carry

            lax.fori_loop(0, N, arrive, 0)

            @pl.when(t < STEPS - 1)
            def _():
                for cc in range(N):
                    line = [delta[r, cc] for r in range(N)]
                    res = apply_line(line, [co[1, fm, p, cc] for p in range(N)])
                    for r in range(N):
                        face[r, cc] = ap[fm, r, cc] + res[r] + diag[r, cc] * line[r]
                for r in range(N):
                    line = [delta[r, cc] for cc in range(N)]
                    res = apply_line(line, [co[2, fm, r, p] for p in range(N)])
                    for cc in range(N):
                        face[r, cc] = face[r, cc] + res[cc]

            def drain(r, carry):
                for j in range(3):
                    z_hop(t, r, j).wait_send()
                    y_hop(t, r, j).wait_send()
                for j in range(2):
                    x_hop(t, r, j).wait_send()
                return carry

            lax.fori_loop(0, N, drain, 0)

        return carry

    lax.fori_loop(0, STEPS, step, 0)
    done = pltpu.make_async_copy(u, out, store_sem)
    done.start()
    done.wait()


def local(field, coeffs, reaction, step_scale, rotation):
    block = field.shape[1:]
    tile = block[-2:]
    f32 = jnp.float32
    dma = pltpu.SemaphoreType.DMA
    table = jnp.asarray(mortar_constants().reshape(-1))
    any_spec = pl.BlockSpec(memory_space=pl.ANY)
    smem_spec = pl.BlockSpec(memory_space=pltpu.SMEM)

    def face_buffers(*lead):
        return pltpu.VMEM((*lead, N, N, *tile), f32)

    result = pl.pallas_call(
        kernel,
        out_shape=jax.ShapeDtypeStruct(block, f32),
        in_specs=[smem_spec, smem_spec, any_spec, any_spec, any_spec, any_spec],
        out_specs=any_spec,
        scratch_shapes=[
            pltpu.VMEM(block, f32),
            pltpu.VMEM((3, *block), f32),
            pltpu.VMEM(block, f32),
            pltpu.VMEM(block, f32),
            pltpu.VMEM(block, f32),
            pltpu.VMEM((STEPS, 2 * N * N, *tile), f32),
            pltpu.VMEM((STEPS, 3, N, *tile), jnp.int32),
            face_buffers(),
            face_buffers(),
            face_buffers(),
            pltpu.VMEM((STEPS, 2, *tile), f32),
            pltpu.VMEM((STEPS, 2, *tile), f32),
            face_buffers(STEPS),
            face_buffers(STEPS),
            face_buffers(STEPS, 3),
            face_buffers(STEPS),
            face_buffers(STEPS, 3),
            face_buffers(STEPS),
            face_buffers(STEPS, 2),
            dma((N, 4)),
            dma,
            dma,
            dma,
            dma((STEPS, 2)),
            dma((STEPS, 2)),
            dma((STEPS,)),
            dma((STEPS,)),
            dma((STEPS, 3, N)),
            dma((STEPS, 3, N)),
            dma((STEPS, 3, N)),
            dma((STEPS, 3, N)),
            dma((STEPS, 2, N)),
            dma((STEPS, 2, N)),
        ],
        compiler_params=pltpu.CompilerParams(
            collective_id=0, has_side_effects=True, vmem_limit_bytes=60 * 1024 * 1024
        ),
    )(rotation, table, field[0], coeffs[0], reaction[0], step_scale[0])
    return result[None]


def solution(mesh):
    in_specs = (
        P("side", None, None, None, None, "circ"),
        P("side", None, None, None, None, None, "circ"),
        P("side", None, None, None, None, "circ"),
        P("side", None, None, None, None, "circ"),
        P(),
    )
    out_specs = P("side", None, None, None, None, "circ")
    return jax.shard_map(local, mesh=mesh, in_specs=in_specs, out_specs=out_specs, check_vma=False)
```

time: 333 us -> 93.5 us (0.28); the launches traced: 328 us -> 93.4 us
  Pallas kernels: 0 us -> 90.8 us
  starting transfers between devices: 90.1 us -> 0 us
  waiting for transfers between devices: 78.5 us -> 0 us
  loops' own time: 60.8 us -> 0 us
  matrix products: 46.7 us -> 0 us
  other arithmetic: 30.1 us -> 0 us
  local copies, waits for them, and re-layouts: 13 us -> 2.53 us
  between operations: 9.08 us -> 0.01 us
    pallas_call x0 -> x1, Pallas kernels: none -> 90.8 us  [local(): pl.pallas_call(kernel, out_shape=jax.ShapeDtypeStruct(block, f32), in_spe...]
    ppermute x28 -> x0, starting transfers between devices: 90.1 us -> none  [the longest x8 47.7 us: padded_2(): lax.ppermute(lax.slice_in_dim(block, 0, width, axis=dim), axis, backward)]
    ppermute x28 -> x0, waiting for transfers between devices: 78.5 us -> none  [the longest x12 52.2 us: passed_along(): return lax.ppermute(value, axis, pairs)]
    another operation x4 -> x0, loops' own time: 60.8 us -> none  [rotate_window(): rotated = lax.switch(sector_k, branches, block)]
    dot_general x32 -> x0, matrix products: 46.7 us -> none  [the longest x4 8.61 us: element_apply(): jnp.einsum('pa,prcxe->arcxe', derivative, coeffs[0] * grad_axial, precisi...]
    scatter-add x24 -> x0, other arithmetic: 17.8 us -> none  [the longest x4 7.4 us: local(): summed = summed.at[:, :, 0].add(padded[1, :, :, :, :-2])]
    scatter-add x4 -> x0, local copies, waits for them, and re-layouts: 6.11 us -> none  [local(): summed = summed.at[:, :, 6].add(padded[0, :, :, :, 2:])]
    another operation x4 -> x0, other arithmetic: 3.79 us -> none  [local(): sector_rims = jnp.stack([applied[:, :, 0], applied[:, :, 6]])]
  transfers between devices with their start and end apart: 28 -> 0, of which waited for: 13 -> 0; matrix products, arithmetic and copies ran while one was open for 8% -> 0% of each run, Pallas kernels for 0% -> 0%
where the time goes in v1:
time: 93.5 us; the launch traced here: 93.4 us
  Pallas kernels  90.8 us (97%)
  local copies, waits for them, and re-layouts  2.53 us (3%)
    pallas_call x1, Pallas kernels, local(): pl.pallas_call(kernel, out_shape=jax.ShapeDtypeStruct(block, f32), in_spe...  90.8 us
    unnamed x1, local copies, waits for them, and re-layouts  2.53 us

profile of v1, /device:TPU:1, one launch (start us, length us, event | category | flops | bytes accessed | tf_op | source)
XLA Modules:
  0.0 93.4 jit_solution(5663929202841074305)
XLA Ops:
  0.0 90.8 %shard_map.64 = f32[7,7,7,8,128]{4,3,2,1,0:T(8,128)} custom-call(s32[4]{0:T(128)} %rot.1, f32[588]{0:T(1024)} %constant.2.clone.table, f32[7,7,7,8,128]{4,3,2,1,0:T(8,128)} %bitcast.7, f32[3,7,7,7,8,128]{5,4,3,2,1,0:T(8,128)} %bitcast.6, f32[7,7,7,8,128]{4,3,2,1,0:T(8,128)} %bitcast.8, f32[7,7,7,8,128]{4,3,2,1,0:T(8,128)} %bitcast.9), custom_call_target="tpu_custom_call" | custom-call | tf_op jit(solution)/shard_map/pallas_call | solution.py:464
  90.8 2.5 %copy.8 = f32[1,7,7,7,8,128]{5,4,3,2,1,0:T(8,128)} copy(f32[1,7,7,7,8,128]{5,4,3,2,1,0:T(8,128)} %bitcast.5) | data formatting | bytes 2809856

commit v2 on v1

--- a/solution.py
+++ b/solution.py
@@ -11,6 +11,7 @@
 N = 7
 NY = 4
 NZ = 4
+SPLIT = 4
 MESH = pl.DeviceIdType.MESH
 
 
@@ -96,13 +97,13 @@
 
 
 def kernel(
-    rot, table, field, coeffs, reaction, scale, out,
-    u, co, re, sc, ap, splat, codes, face, delta, diag,
+    rot, table, field, coeffs, reaction, scale, u,
+    co, re, sc, ap, splat, codes, face, delta, diag,
     halo_src, halo_dst, side_dst,
-    zsrc, zdst, ysrc, ydst, xsrc, xdst,
-    load_u, load_c, load_s, store_sem,
+    src1, dst1, src2, dst2, src3, dst3,
+    load_u, load_c, load_s,
     halo_send, halo_recv, side_send, side_recv,
-    zsend, zrecv, ysend, yrecv, xsend, xrecv,
+    send1, recv1, send2, recv2, send3, recv3,
 ):
     c = lax.axis_index("circ")
     side = lax.axis_index("side")
@@ -129,15 +130,18 @@
     x_dev = [at((x_me + j) % 2, y_me, z_me) for j in range(2)]
     across = 3 - side
 
+    def ordered(i):
+        return jnp.where(parity == 1, 6 - i, i)
+
     def load_slice(a):
         return [
-            pltpu.make_async_copy(field.at[a], u.at[a], load_u.at[a, 0]),
-            pltpu.make_async_copy(reaction.at[a], re.at[a], load_u.at[a, 1]),
-            pltpu.make_async_copy(coeffs.at[1, a], co.at[1, a], load_u.at[a, 2]),
-            pltpu.make_async_copy(coeffs.at[2, a], co.at[2, a], load_u.at[a, 3]),
+            pltpu.make_async_copy(reaction.at[a], re.at[a], load_u.at[a, 0]),
+            pltpu.make_async_copy(coeffs.at[1, a], co.at[1, a], load_u.at[a, 1]),
+            pltpu.make_async_copy(coeffs.at[2, a], co.at[2, a], load_u.at[a, 2]),
         ]
 
-    load_axial = pltpu.make_async_copy(coeffs.at[0], co.at[0], load_c)
+    load_field = pltpu.make_async_copy(field, u, load_c.at[0])
+    load_axial = pltpu.make_async_copy(coeffs.at[0], co.at[0], load_c.at[1])
     load_scale = pltpu.make_async_copy(scale, sc, load_s)
 
     barrier = pltpu.get_barrier_semaphore()
@@ -158,22 +162,28 @@
         for d in x_dev:
             greet(d, across)
 
-    def issue(a, carry):
-        for copy in load_slice(a):
+    load_field.start()
+    for copy in load_slice(fm):
+        copy.start()
+    load_axial.start()
+
+    def issue(i, carry):
+        for copy in load_slice(ordered(i)):
             copy.start()
         return carry
 
-    lax.fori_loop(0, N, issue, 0)
-    load_axial.start()
+    lax.fori_loop(1, N, issue, 0)
     load_scale.start()
 
     def digits(shift):
         s = shift & 127
         total = ((shift >> 7) + jnp.where(lane < s, 1, 0)) & 31
         dz = total & 3
-        dy = ((total >> 2) & 3) + jnp.where(z_me < dz, 1, 0)
-        dx = ((total >> 4) + jnp.where(y_me < dy, 1, 0)) & 1
-        return dz, dy & 3, dx
+        dy = (total >> 2) & 3
+        late = dy + jnp.where(z_me < dz, 1, 0)
+        early = dy + jnp.where(z_me + dz > 3, 1, 0)
+        dx = ((total >> 4) + jnp.where(y_me < late, 1, 0)) & 1
+        return dz, early & 3, late & 3, dx
 
     @pl.when(is_mortar)
     def _():
@@ -187,10 +197,11 @@
                 kappa = k + jnp.where(m < left, 1, 0)
                 kappa = jnp.where(kappa >= cycle, kappa - cycle, kappa)
                 back = jnp.where(kappa == 0, 0, cycle - kappa)
-                dz, dy, _ = digits(jnp.where(is_rotor, kappa, back))
+                dz, early, late, _ = digits(jnp.where(is_rotor, kappa, back))
                 codes[t, 0, m] = dz
-                codes[t, 1, m] = dy
-                codes[t, 2, m] = digits(jnp.where(is_rotor, back, kappa))[2]
+                codes[t, 1, m] = early
+                codes[t, 2, m] = late
+                codes[t, 3, m] = digits(jnp.where(is_rotor, back, kappa))[3]
             half = jnp.where(is_rotor, 0, 1)
             first = (half * SUBSTEPS + residue) * 2 * N * N
             for i in range(2 * N * N):
@@ -219,34 +230,27 @@
                 ap[a, r, cc] = ap[a, r, cc] + res[a]
         return carry
 
-    def first_slice(a, carry):
-        for copy in load_slice(a):
-            copy.wait()
-        in_face(a)
-        return carry
-
     def next_slice(a, carry):
         in_face(a)
         return carry
 
-    lax.fori_loop(0, N, first_slice, 0)
+    edge = [jnp.where(parity == 1, float(DERIV[p, 6]), float(DERIV[p, 0])) for p in range(N)]
+
+    load_field.wait()
+    for copy in load_slice(fm):
+        copy.wait()
+    in_face(fm)
     load_axial.wait()
-    lax.fori_loop(0, N, axial, 0)
-    load_scale.wait()
-
-    edge = [jnp.where(parity == 1, float(DERIV[p, 6]), float(DERIV[p, 0])) for p in range(N)]
 
     @pl.when(is_mortar)
     def _():
         def body(r, carry):
             for cc in range(N):
-                total = re[fm, r, cc]
+                grad = half_line(DERIV, [u[a, r, cc] for a in range(N)])
+                total = ap[fm, r, cc]
                 for p in range(N):
-                    total = total + float(DERIV[p, 0]) ** 2 * jnp.where(
-                        parity == 1, co[0, 6 - p, r, cc], co[0, p, r, cc]
-                    )
-                diag[r, cc] = total
-                face[r, cc] = ap[fm, r, cc]
+                    total = total + edge[p] * (co[0, p, r, cc] * grad[p])
+                face[r, cc] = total
             return carry
 
         lax.fori_loop(0, N, body, 0)
@@ -265,14 +269,24 @@
             device_id={"circ": cc, "side": ss}, device_id_type=MESH,
         )
 
-    def z_hop(t, r, j):
-        return hop(zsrc.at[t, r], zdst.at[t, j, r], zsend.at[t, j, r], zrecv.at[t, j, r], z_dev[j], side)
-
-    def y_hop(t, r, j):
-        return hop(ysrc.at[t, r], ydst.at[t, j, r], ysend.at[t, j, r], yrecv.at[t, j, r], y_dev[j], side)
-
-    def x_hop(t, r, j):
-        return hop(xsrc.at[t, r], xdst.at[t, j, r], xsend.at[t, j, r], xrecv.at[t, j, r], x_dev[j], across)
+    def mixed(i):
+        return i // 2 + SPLIT * (i % 2)
+
+    def first_hop(t, r, j):
+        dev = jnp.where(r < SPLIT, z_dev[j], y_dev[j])
+        return hop(src1.at[t, r], dst1.at[t, j, r], send1.at[t, j, r], recv1.at[t, j, r], dev, side)
+
+    def second_hop(t, r, j):
+        dev = jnp.where(r < SPLIT, y_dev[j], z_dev[j])
+        return hop(src2.at[t, r], dst2.at[t, j, r], send2.at[t, j, r], recv2.at[t, j, r], dev, side)
+
+    def last_hop(t, r, j):
+        return hop(src3.at[t, r], dst3.at[t, j, r], send3.at[t, j, r], recv3.at[t, j, r], x_dev[j], across)
+
+    def pick(code, own, others):
+        low = jnp.where(code == 0, own, others[0])
+        high = jnp.where(code == 2, others[1], others[2])
+        return jnp.where(code < 2, low, high)
 
     def step(t, carry):
         @pl.when(is_mortar)
@@ -286,15 +300,16 @@
                 kappa = k + jnp.where(m < left, 1, 0)
                 shifts.append(jnp.where(is_rotor, kappa, 128 * 64 - kappa) & 127)
 
-            def send(r, carry):
+            def send(i, carry):
+                r = mixed(i)
                 nodes = [face[r, n] for n in range(N)]
                 for m in range(N):
                     total = splat[t, m * N] * nodes[0]
                     for n in range(1, N):
                         total = total + splat[t, m * N + n] * nodes[n]
-                    zsrc[t, r, m] = pltpu.roll(total, shifts[m], 1)
+                    src1[t, r, m] = pltpu.roll(total, shifts[m], 1)
                 for j in range(3):
-                    z_hop(t, r, j).start()
+                    first_hop(t, r, j).start()
                 return carry
 
             lax.fori_loop(0, N, send, 0)
@@ -313,6 +328,33 @@
 
                 lax.fori_loop(0, N, rest, 0)
 
+        @pl.when(t == 0)
+        def _():
+            def first_slice(i, carry):
+                a = ordered(i)
+                for copy in load_slice(a):
+                    copy.wait()
+                in_face(a)
+                return carry
+
+            lax.fori_loop(1, N, first_slice, 0)
+            lax.fori_loop(0, N, axial, 0)
+            load_scale.wait()
+
+            @pl.when(is_mortar)
+            def _():
+                def body(r, carry):
+                    for cc in range(N):
+                        total = re[fm, r, cc]
+                        for p in range(N):
+                            total = total + float(DERIV[p, 0]) ** 2 * jnp.where(
+                                parity == 1, co[0, 6 - p, r, cc], co[0, p, r, cc]
+                            )
+                        diag[r, cc] = total
+                    return carry
+
+                lax.fori_loop(0, N, body, 0)
+
         side_copy = hop(ap.at[fp], side_dst.at[t], side_send.at[t], side_recv.at[t], c, partner)
         side_copy.start()
 
@@ -332,6 +374,24 @@
         high_copy = hop(halo_src.at[t, 1], halo_dst.at[t, 1], halo_send.at[t, 1], halo_recv.at[t, 1], nxt, side)
         low_copy.start()
         high_copy.start()
+
+        @pl.when(is_mortar)
+        def _():
+            def first_relay(i, carry):
+                r = mixed(i)
+                for j in range(3):
+                    first_hop(t, r, j).wait_recv()
+                which = jnp.where(r < SPLIT, 0, 1)
+                for m in range(N):
+                    src2[t, r, m] = pick(
+                        codes[t, which, m], src1[t, r, m], [dst1[t, j, r, m] for j in range(3)]
+                    )
+                for j in range(3):
+                    second_hop(t, r, j).start()
+                return carry
+
+            lax.fori_loop(0, N, first_relay, 0)
+
         low_copy.wait()
         high_copy.wait()
 
@@ -363,48 +423,40 @@
 
         lax.fori_loop(0, N, add_side, 0)
 
+        def relay(i, carry):
+            @pl.when(is_mortar)
+            def _():
+                r = mixed(i)
+                for j in range(3):
+                    second_hop(t, r, j).wait_recv()
+                which = jnp.where(r < SPLIT, 2, 0)
+                for m in range(N):
+                    src3[t, r, m] = pick(
+                        codes[t, which, m], src2[t, r, m], [dst2[t, j, r, m] for j in range(3)]
+                    )
+                for j in range(2):
+                    last_hop(t, r, j).start()
+
+            @pl.when(t < STEPS - 1)
+            def _():
+                in_face(i)
+
+            return carry
+
+        lax.fori_loop(0, N, relay, 0)
+
+        @pl.when(t < STEPS - 1)
+        def _():
+            lax.fori_loop(0, N, axial, 0)
+
         @pl.when(is_mortar)
         def _():
-            def along_y(r, carry):
-                for j in range(3):
-                    z_hop(t, r, j).wait_recv()
-                for m in range(N):
-                    code = codes[t, 0, m]
-                    low = jnp.where(code == 0, zsrc[t, r, m], zdst[t, 0, r, m])
-                    high = jnp.where(code == 2, zdst[t, 1, r, m], zdst[t, 2, r, m])
-                    ysrc[t, r, m] = jnp.where(code < 2, low, high)
-                for j in range(3):
-                    y_hop(t, r, j).start()
-                return carry
-
-            lax.fori_loop(0, N, along_y, 0)
-
-            def along_x(r, carry):
-                for j in range(3):
-                    y_hop(t, r, j).wait_recv()
-                for m in range(N):
-                    code = codes[t, 1, m]
-                    low = jnp.where(code == 0, ysrc[t, r, m], ydst[t, 0, r, m])
-                    high = jnp.where(code == 2, ydst[t, 1, r, m], ydst[t, 2, r, m])
-                    xsrc[t, r, m] = jnp.where(code < 2, low, high)
+            def arrive(i, carry):
+                r = mixed(i)
                 for j in range(2):
-                    x_hop(t, r, j).start()
-                return carry
-
-            lax.fori_loop(0, N, along_x, 0)
-
-        @pl.when(t < STEPS - 1)
-        def _():
-            lax.fori_loop(0, N, next_slice, 0)
-            lax.fori_loop(0, N, axial, 0)
-
-        @pl.when(is_mortar)
-        def _():
-            def arrive(r, carry):
-                for j in range(2):
-                    x_hop(t, r, j).wait_recv()
+                    last_hop(t, r, j).wait_recv()
                 nodes = [
-                    jnp.where(codes[t, 2, m] == 0, xdst[t, 0, r, m], xdst[t, 1, r, m])
+                    jnp.where(codes[t, 3, m] == 0, dst3[t, 0, r, m], dst3[t, 1, r, m])
                     for m in range(N)
                 ]
                 for n in range(N):
@@ -433,10 +485,10 @@
 
             def drain(r, carry):
                 for j in range(3):
-                    z_hop(t, r, j).wait_send()
-                    y_hop(t, r, j).wait_send()
+                    first_hop(t, r, j).wait_send()
+                    second_hop(t, r, j).wait_send()
                 for j in range(2):
-                    x_hop(t, r, j).wait_send()
+                    last_hop(t, r, j).wait_send()
                 return carry
 
             lax.fori_loop(0, N, drain, 0)
@@ -444,9 +496,6 @@
         return carry
 
     lax.fori_loop(0, STEPS, step, 0)
-    done = pltpu.make_async_copy(u, out, store_sem)
-    done.start()
-    done.wait()
 
 
 def local(field, coeffs, reaction, step_scale, rotation):
@@ -455,7 +504,7 @@
     f32 = jnp.float32
     dma = pltpu.SemaphoreType.DMA
     table = jnp.asarray(mortar_constants().reshape(-1))
-    any_spec = pl.BlockSpec(memory_space=pl.ANY)
+    hbm_spec = pl.BlockSpec(memory_space=pltpu.HBM)
     smem_spec = pl.BlockSpec(memory_space=pltpu.SMEM)
 
     def face_buffers(*lead):
@@ -463,17 +512,16 @@
 
     result = pl.pallas_call(
         kernel,
-        out_shape=jax.ShapeDtypeStruct(block, f32),
-        in_specs=[smem_spec, smem_spec, any_spec, any_spec, any_spec, any_spec],
-        out_specs=any_spec,
+        out_shape=pltpu.VMEM(block, f32),
+        in_specs=[smem_spec, smem_spec, hbm_spec, hbm_spec, hbm_spec, hbm_spec],
+        out_specs=pl.BlockSpec(memory_space=pltpu.VMEM),
         scratch_shapes=[
-            pltpu.VMEM(block, f32),
             pltpu.VMEM((3, *block), f32),
             pltpu.VMEM(block, f32),
             pltpu.VMEM(block, f32),
             pltpu.VMEM(block, f32),
             pltpu.VMEM((STEPS, 2 * N * N, *tile), f32),
-            pltpu.VMEM((STEPS, 3, N, *tile), jnp.int32),
+            pltpu.VMEM((STEPS, 4, N, *tile), jnp.int32),
             face_buffers(),
             face_buffers(),
             face_buffers(),
@@ -486,9 +534,8 @@
             face_buffers(STEPS, 3),
             face_buffers(STEPS),
             face_buffers(STEPS, 2),
-            dma((N, 4)),
-            dma,
-            dma,
+            dma((N, 3)),
+            dma((2,)),
             dma,
             dma((STEPS, 2)),
             dma((STEPS, 2)),
@@ -502,7 +549,7 @@
             dma((STEPS, 2, N)),
         ],
         compiler_params=pltpu.CompilerParams(
-            collective_id=0, has_side_effects=True, vmem_limit_bytes=60 * 1024 * 1024
+            collective_id=0, has_side_effects=True, vmem_limit_bytes=61 * 1024 * 1024
         ),
     )(rotation, table, field[0], coeffs[0], reaction[0], step_scale[0])
     return result[None]

time: 93.5 us -> 69.5 us (0.74)
  Pallas kernels: 90.8 us -> 68.3 us
  local copies, waits for them, and re-layouts: 2.53 us -> 1.09 us
    pallas_call x1, Pallas kernels: 90.8 us -> 68.3 us  [local(): pl.pallas_call(kernel, out_shape=pltpu.VMEM(block, f32), in_specs=[smem_s...]
    unnamed x1, local copies, waits for them, and re-layouts: 2.53 us -> 1.09 us
where the time goes in v2:
time: 69.5 us; the launch traced here: 69.4 us
  Pallas kernels  68.3 us (98%)
  local copies, waits for them, and re-layouts  1.09 us (2%)
    pallas_call x1, Pallas kernels, local(): pl.pallas_call(kernel, out_shape=pltpu.VMEM(block, f32), in_specs=[smem_s...  68.3 us

profile of v2, /device:TPU:1, one launch (start us, length us, event | category | flops | bytes accessed | tf_op | source)
XLA Modules:
  0.0 69.4 jit_solution(2553484714312310872)
XLA Ops:
  0.0 68.3 %shard_map.64 = f32[7,7,7,8,128]{4,3,2,1,0:T(8,128)S(1)} custom-call(s32[4]{0:T(128)} %rot.1, f32[588]{0:T(1024)} %constant.2.clone.table, f32[7,7,7,8,128]{4,3,2,1,0:T(8,128)} %bitcast.7, f32[3,7,7,7,8,128]{5,4,3,2,1,0:T(8,128)} %bitcast.6, f32[7,7,7,8,128]{4,3,2,1,0:T(8,128)} %bitcast.8, f32[7,7,7,8,128]{4,3,2,1,0:T(8,128)} %bitcast.9), custom_call_target="tpu_custom_call" | custom-call | tf_op jit(solution)/shard_map/pallas_call | solution.py:513
  68.3 1.1 %copy.8 = f32[1,7,7,7,8,128]{5,4,3,2,1,0:T(8,128)} copy(f32[1,7,7,7,8,128]{5,4,3,2,1,0:T(8,128)S(1)} %bitcast.5) | data formatting | bytes 2809856

commit v3 on v2

--- a/solution.py
+++ b/solution.py
@@ -11,7 +11,7 @@
 N = 7
 NY = 4
 NZ = 4
-SPLIT = 4
+PIECES = ((0, 4), (4, 3))
 MESH = pl.DeviceIdType.MESH
 
 
@@ -103,7 +103,7 @@
     src1, dst1, src2, dst2, src3, dst3,
     load_u, load_c, load_s,
     halo_send, halo_recv, side_send, side_recv,
-    send1, recv1, send2, recv2, send3, recv3,
+    send0, recv0, send1, recv1, send2, recv2, send3, recv3,
 ):
     c = lax.axis_index("circ")
     side = lax.axis_index("side")
@@ -111,9 +111,10 @@
     z_me = c % NZ
     y_me = (c // NZ) % NY
     x_me = c // (NZ * NY)
+    parity = side % 2
     is_mortar = (side == 1) | (side == 2)
+    is_relay = parity == 1
     is_rotor = side < 2
-    parity = side % 2
     partner = side + 1 - 2 * parity
     fp = 6 - 6 * parity
     fm = 6 * parity
@@ -128,7 +129,8 @@
     z_dev = [at(x_me, y_me, (z_me + j + 1) % NZ) for j in range(3)]
     y_dev = [at(x_me, (y_me + j + 1) % NY, z_me) for j in range(3)]
     x_dev = [at((x_me + j) % 2, y_me, z_me) for j in range(2)]
-    across = 3 - side
+    first_side = jnp.where(side == 1, 1, 3)
+    last_side = jnp.where(side == 1, 2, 1)
 
     def ordered(i):
         return jnp.where(parity == 1, 6 - i, i)
@@ -155,12 +157,21 @@
     greet(prv, side)
     greet(c, partner)
 
-    @pl.when(is_mortar)
-    def _():
-        for d in z_dev + y_dev:
-            greet(d, side)
-        for d in x_dev:
-            greet(d, across)
+    ring = z_dev + y_dev
+    peers = {
+        1: [(d, 1) for d in ring] + [(d, 2) for d in x_dev] + [(d, 3) for d in x_dev],
+        2: [(d, 3) for d in ring] + [(d, 1) for d in x_dev],
+        3: [(d, 2) for d in ring] + [(d, 3) for d in ring] + [(d, 1) for d in x_dev],
+    }
+
+    def greet_peers(which):
+        @pl.when(side == which)
+        def _():
+            for d, ss in peers[which]:
+                greet(d, ss)
+
+    for which in peers:
+        greet_peers(which)
 
     load_field.start()
     for copy in load_slice(fm):
@@ -185,7 +196,7 @@
         dx = ((total >> 4) + jnp.where(y_me < late, 1, 0)) & 1
         return dz, early & 3, late & 3, dx
 
-    @pl.when(is_mortar)
+    @pl.when(side > 0)
     def _():
         def prepare(t, carry):
             offset = rot[t]
@@ -255,13 +266,13 @@
 
         lax.fori_loop(0, N, body, 0)
 
-    @pl.when(is_mortar)
-    def _():
-        pl.semaphore_wait(barrier, 11)
-
-    @pl.when(jnp.logical_not(is_mortar))
-    def _():
-        pl.semaphore_wait(barrier, 3)
+    def meet(which):
+        @pl.when(side == which)
+        def _():
+            pl.semaphore_wait(barrier, 3 + len(peers.get(which, [])))
+
+    for which in range(4):
+        meet(which)
 
     def hop(src, dst, send, recv, cc, ss):
         return pltpu.make_async_remote_copy(
@@ -269,19 +280,28 @@
             device_id={"circ": cc, "side": ss}, device_id_type=MESH,
         )
 
-    def mixed(i):
-        return i // 2 + SPLIT * (i % 2)
-
-    def first_hop(t, r, j):
-        dev = jnp.where(r < SPLIT, z_dev[j], y_dev[j])
-        return hop(src1.at[t, r], dst1.at[t, j, r], send1.at[t, j, r], recv1.at[t, j, r], dev, side)
-
-    def second_hop(t, r, j):
-        dev = jnp.where(r < SPLIT, y_dev[j], z_dev[j])
-        return hop(src2.at[t, r], dst2.at[t, j, r], send2.at[t, j, r], recv2.at[t, j, r], dev, side)
-
-    def last_hop(t, r, j):
-        return hop(src3.at[t, r], dst3.at[t, j, r], send3.at[t, j, r], recv3.at[t, j, r], x_dev[j], across)
+    def nodes_of(h):
+        return pl.ds(*PIECES[h])
+
+    def z_first(r, h):
+        return r % 2 == h
+
+    def first_hop(t, r, h, j):
+        dev = jnp.where(z_first(r, h), z_dev[j], y_dev[j])
+        return hop(src1.at[t, r, nodes_of(h)], dst1.at[t, j, r, nodes_of(h)],
+                   send1.at[t, j, r, h], recv1.at[t, j, r, h], dev, first_side)
+
+    def own_hop(t, r):
+        return hop(src1.at[t, r], src1.at[t, r], send0.at[t, r], recv0.at[t, r], c, partner)
+
+    def second_hop(t, r, h, j):
+        dev = jnp.where(z_first(r, h), y_dev[j], z_dev[j])
+        return hop(src2.at[t, r, nodes_of(h)], dst2.at[t, j, r, nodes_of(h)],
+                   send2.at[t, j, r, h], recv2.at[t, j, r, h], dev, side)
+
+    def last_hop(t, r, h, j):
+        return hop(src3.at[t, r, nodes_of(h)], dst3.at[t, j, r, nodes_of(h)],
+                   send3.at[t, j, r, h], recv3.at[t, j, r, h], x_dev[j], last_side)
 
     def pick(code, own, others):
         low = jnp.where(code == 0, own, others[0])
@@ -300,16 +320,21 @@
                 kappa = k + jnp.where(m < left, 1, 0)
                 shifts.append(jnp.where(is_rotor, kappa, 128 * 64 - kappa) & 127)
 
-            def send(i, carry):
-                r = mixed(i)
+            def send(r, carry):
                 nodes = [face[r, n] for n in range(N)]
                 for m in range(N):
                     total = splat[t, m * N] * nodes[0]
                     for n in range(1, N):
                         total = total + splat[t, m * N + n] * nodes[n]
                     src1[t, r, m] = pltpu.roll(total, shifts[m], 1)
-                for j in range(3):
-                    first_hop(t, r, j).start()
+                for h in range(2):
+                    for j in range(3):
+                        first_hop(t, r, h, j).start()
+
+                @pl.when(side == 2)
+                def _():
+                    own_hop(t, r).start()
+
                 return carry
 
             lax.fori_loop(0, N, send, 0)
@@ -375,19 +400,23 @@
         low_copy.start()
         high_copy.start()
 
-        @pl.when(is_mortar)
-        def _():
-            def first_relay(i, carry):
-                r = mixed(i)
-                for j in range(3):
-                    first_hop(t, r, j).wait_recv()
-                which = jnp.where(r < SPLIT, 0, 1)
-                for m in range(N):
-                    src2[t, r, m] = pick(
-                        codes[t, which, m], src1[t, r, m], [dst1[t, j, r, m] for j in range(3)]
-                    )
-                for j in range(3):
-                    second_hop(t, r, j).start()
+        @pl.when(is_relay)
+        def _():
+            def first_relay(r, carry):
+                @pl.when(side == 3)
+                def _():
+                    own_hop(t, r).wait_recv()
+
+                for h in range(2):
+                    for j in range(3):
+                        first_hop(t, r, h, j).wait_recv()
+                    which = jnp.where(z_first(r, h), 0, 1)
+                    for m in range(PIECES[h][0], sum(PIECES[h])):
+                        src2[t, r, m] = pick(
+                            codes[t, which, m], src1[t, r, m], [dst1[t, j, r, m] for j in range(3)]
+                        )
+                    for j in range(3):
+                        second_hop(t, r, h, j).start()
                 return carry
 
             lax.fori_loop(0, N, first_relay, 0)
@@ -423,23 +452,23 @@
 
         lax.fori_loop(0, N, add_side, 0)
 
-        def relay(i, carry):
-            @pl.when(is_mortar)
+        def relay(r, carry):
+            @pl.when(is_relay)
             def _():
-                r = mixed(i)
-                for j in range(3):
-                    second_hop(t, r, j).wait_recv()
-                which = jnp.where(r < SPLIT, 2, 0)
-                for m in range(N):
-                    src3[t, r, m] = pick(
-                        codes[t, which, m], src2[t, r, m], [dst2[t, j, r, m] for j in range(3)]
-                    )
-                for j in range(2):
-                    last_hop(t, r, j).start()
+                for h in range(2):
+                    for j in range(3):
+                        second_hop(t, r, h, j).wait_recv()
+                    which = jnp.where(z_first(r, h), 2, 0)
+                    for m in range(PIECES[h][0], sum(PIECES[h])):
+                        src3[t, r, m] = pick(
+                            codes[t, which, m], src2[t, r, m], [dst2[t, j, r, m] for j in range(3)]
+                        )
+                    for j in range(2):
+                        last_hop(t, r, h, j).start()
 
             @pl.when(t < STEPS - 1)
             def _():
-                in_face(i)
+                in_face(r)
 
             return carry
 
@@ -451,21 +480,30 @@
 
         @pl.when(is_mortar)
         def _():
-            def arrive(i, carry):
-                r = mixed(i)
-                for j in range(2):
-                    last_hop(t, r, j).wait_recv()
+            def arrive(r, carry):
+                for h in range(2):
+                    for j in range(2):
+                        last_hop(t, r, h, j).wait_recv()
                 nodes = [
                     jnp.where(codes[t, 3, m] == 0, dst3[t, 0, r, m], dst3[t, 1, r, m])
                     for m in range(N)
                 ]
+                changes = []
                 for n in range(N):
                     total = splat[t, N * N + n * N] * nodes[0]
                     for m in range(1, N):
                         total = total + splat[t, N * N + n * N + m] * nodes[m]
                     change = -(sc[fm, r, n] * total)
+                    changes.append(change)
                     delta[r, n] = change
                     u[fm, r, n] = u[fm, r, n] + change
+
+                @pl.when(t < STEPS - 1)
+                def _():
+                    res = apply_line(changes, [co[2, fm, r, p] for p in range(N)])
+                    for n in range(N):
+                        face[r, n] = ap[fm, r, n] + res[n] + diag[r, n] * changes[n]
+
                 return carry
 
             lax.fori_loop(0, N, arrive, 0)
@@ -476,26 +514,37 @@
                     line = [delta[r, cc] for r in range(N)]
                     res = apply_line(line, [co[1, fm, p, cc] for p in range(N)])
                     for r in range(N):
-                        face[r, cc] = ap[fm, r, cc] + res[r] + diag[r, cc] * line[r]
-                for r in range(N):
-                    line = [delta[r, cc] for cc in range(N)]
-                    res = apply_line(line, [co[2, fm, r, p] for p in range(N)])
-                    for cc in range(N):
-                        face[r, cc] = face[r, cc] + res[cc]
-
-            def drain(r, carry):
+                        face[r, cc] = face[r, cc] + res[r]
+
+        return carry
+
+    lax.fori_loop(0, STEPS, step, 0)
+
+    def drain(i, carry):
+        t = i // N
+        r = i % N
+
+        @pl.when(is_mortar)
+        def _():
+            for h in range(2):
                 for j in range(3):
-                    first_hop(t, r, j).wait_send()
-                    second_hop(t, r, j).wait_send()
+                    first_hop(t, r, h, j).wait_send()
+
+        @pl.when(side == 2)
+        def _():
+            own_hop(t, r).wait_send()
+
+        @pl.when(is_relay)
+        def _():
+            for h in range(2):
+                for j in range(3):
+                    second_hop(t, r, h, j).wait_send()
                 for j in range(2):
-                    last_hop(t, r, j).wait_send()
-                return carry
-
-            lax.fori_loop(0, N, drain, 0)
+                    last_hop(t, r, h, j).wait_send()
 
         return carry
 
-    lax.fori_loop(0, STEPS, step, 0)
+    lax.fori_loop(0, STEPS * N, drain, 0)
 
 
 def local(field, coeffs, reaction, step_scale, rotation):
@@ -541,12 +590,14 @@
             dma((STEPS, 2)),
             dma((STEPS,)),
             dma((STEPS,)),
-            dma((STEPS, 3, N)),
-            dma((STEPS, 3, N)),
-            dma((STEPS, 3, N)),
-            dma((STEPS, 3, N)),
-            dma((STEPS, 2, N)),
-            dma((STEPS, 2, N)),
+            dma((STEPS, N)),
+            dma((STEPS, N)),
+            dma((STEPS, 3, N, 2)),
+            dma((STEPS, 3, N, 2)),
+            dma((STEPS, 3, N, 2)),
+            dma((STEPS, 3, N, 2)),
+            dma((STEPS, 2, N, 2)),
+            dma((STEPS, 2, N, 2)),
         ],
         compiler_params=pltpu.CompilerParams(
             collective_id=0, has_side_effects=True, vmem_limit_bytes=61 * 1024 * 1024

time: 69.5 us -> 70 us (level)
  no operation moved by 1% of the time
where the time goes in v3:
time: 70 us; the launch traced here: 69.9 us
  Pallas kernels  68.8 us (98%)
  local copies, waits for them, and re-layouts  1.09 us (2%)
    pallas_call x1, Pallas kernels, local(): pl.pallas_call(kernel, out_shape=pltpu.VMEM(block, f32), in_specs=[smem_s...  68.8 us

profile of v3, /device:TPU:1, one launch (start us, length us, event | category | flops | bytes accessed | tf_op | source)
XLA Modules:
  0.0 69.9 jit_solution(12908817889496471485)
XLA Ops:
  0.0 68.8 %shard_map.64 = f32[7,7,7,8,128]{4,3,2,1,0:T(8,128)S(1)} custom-call(s32[4]{0:T(128)} %rot.1, f32[588]{0:T(1024)} %constant.2.clone.table, f32[7,7,7,8,128]{4,3,2,1,0:T(8,128)} %bitcast.7, f32[3,7,7,7,8,128]{5,4,3,2,1,0:T(8,128)} %bitcast.6, f32[7,7,7,8,128]{4,3,2,1,0:T(8,128)} %bitcast.8, f32[7,7,7,8,128]{4,3,2,1,0:T(8,128)} %bitcast.9), custom_call_target="tpu_custom_call" | custom-call | tf_op jit(solution)/shard_map/pallas_call | solution.py:562
  68.8 1.1 %copy.8 = f32[1,7,7,7,8,128]{5,4,3,2,1,0:T(8,128)} copy(f32[1,7,7,7,8,128]{5,4,3,2,1,0:T(8,128)S(1)} %bitcast.5) | data formatting | bytes 2809856

commit v4 on v3

--- a/solution.py
+++ b/solution.py
@@ -100,10 +100,9 @@
     rot, table, field, coeffs, reaction, scale, u,
     co, re, sc, ap, splat, codes, face, delta, diag,
     halo_src, halo_dst, side_dst,
-    src1, dst1, src2, dst2, src3, dst3,
-    load_u, load_c, load_s,
-    halo_send, halo_recv, side_send, side_recv,
-    send0, recv0, send1, recv1, send2, recv2, send3, recv3,
+    dst1, src2, dst2, src3, dst3,
+    load_sem, halo_send, halo_recv, side_send, side_recv,
+    sends, recv1, recv2, recv3,
 ):
     c = lax.axis_index("circ")
     side = lax.axis_index("side")
@@ -135,16 +134,23 @@
     def ordered(i):
         return jnp.where(parity == 1, 6 - i, i)
 
-    def load_slice(a):
-        return [
-            pltpu.make_async_copy(reaction.at[a], re.at[a], load_u.at[a, 0]),
-            pltpu.make_async_copy(coeffs.at[1, a], co.at[1, a], load_u.at[a, 1]),
-            pltpu.make_async_copy(coeffs.at[2, a], co.at[2, a], load_u.at[a, 2]),
-        ]
-
-    load_field = pltpu.make_async_copy(field, u, load_c.at[0])
-    load_axial = pltpu.make_async_copy(coeffs.at[0], co.at[0], load_c.at[1])
-    load_scale = pltpu.make_async_copy(scale, sc, load_s)
+    rest_of = pl.ds(1 - parity, N - 1)
+    in_layer = pl.ds(1, 2)
+
+    def load(i, src, dst):
+        return pltpu.make_async_copy(src, dst, load_sem.at[i])
+
+    load_first = [
+        load(0, field, u),
+        load(1, coeffs.at[in_layer, fm], co.at[in_layer, fm]),
+        load(2, reaction.at[fm], re.at[fm]),
+    ]
+    load_axial = load(3, coeffs.at[0], co.at[0])
+    load_rest = [
+        load(4, coeffs.at[in_layer, rest_of], co.at[in_layer, rest_of]),
+        load(5, reaction.at[rest_of], re.at[rest_of]),
+        load(6, scale, sc),
+    ]
 
     barrier = pltpu.get_barrier_semaphore()
 
@@ -173,18 +179,8 @@
     for which in peers:
         greet_peers(which)
 
-    load_field.start()
-    for copy in load_slice(fm):
+    for copy in load_first + [load_axial] + load_rest:
         copy.start()
-    load_axial.start()
-
-    def issue(i, carry):
-        for copy in load_slice(ordered(i)):
-            copy.start()
-        return carry
-
-    lax.fori_loop(1, N, issue, 0)
-    load_scale.start()
 
     def digits(shift):
         s = shift & 127
@@ -247,8 +243,7 @@
 
     edge = [jnp.where(parity == 1, float(DERIV[p, 6]), float(DERIV[p, 0])) for p in range(N)]
 
-    load_field.wait()
-    for copy in load_slice(fm):
+    for copy in load_first:
         copy.wait()
     in_face(fm)
     load_axial.wait()
@@ -288,20 +283,27 @@
 
     def first_hop(t, r, h, j):
         dev = jnp.where(z_first(r, h), z_dev[j], y_dev[j])
-        return hop(src1.at[t, r, nodes_of(h)], dst1.at[t, j, r, nodes_of(h)],
-                   send1.at[t, j, r, h], recv1.at[t, j, r, h], dev, first_side)
-
-    def own_hop(t, r):
-        return hop(src1.at[t, r], src1.at[t, r], send0.at[t, r], recv0.at[t, r], c, partner)
+        return hop(dst1.at[t, 3, r, nodes_of(h)], dst1.at[t, j, r, nodes_of(h)],
+                   sends.at[0], recv1.at[t % 2, r, h], dev, first_side)
+
+    def own_hop(t, r, h):
+        return hop(dst1.at[t, 3, r, nodes_of(h)], dst1.at[t, 3, r, nodes_of(h)],
+                   sends.at[1], recv1.at[t % 2, r, h], c, partner)
 
     def second_hop(t, r, h, j):
         dev = jnp.where(z_first(r, h), y_dev[j], z_dev[j])
         return hop(src2.at[t, r, nodes_of(h)], dst2.at[t, j, r, nodes_of(h)],
-                   send2.at[t, j, r, h], recv2.at[t, j, r, h], dev, side)
+                   sends.at[2], recv2.at[t % 2, r, h], dev, side)
 
     def last_hop(t, r, h, j):
         return hop(src3.at[t, r, nodes_of(h)], dst3.at[t, j, r, nodes_of(h)],
-                   send3.at[t, j, r, h], recv3.at[t, j, r, h], x_dev[j], last_side)
+                   sends.at[3], recv3.at[t % 2, r], x_dev[j], last_side)
+
+    def landed(ref, sem):
+        hop(ref, ref, sends.at[0], sem, c, partner).wait_recv()
+
+    def sent(ref, i):
+        hop(ref, ref, sends.at[i], recv3.at[0, 0], c, partner).wait_send()
 
     def pick(code, own, others):
         low = jnp.where(code == 0, own, others[0])
@@ -326,14 +328,15 @@
                     total = splat[t, m * N] * nodes[0]
                     for n in range(1, N):
                         total = total + splat[t, m * N + n] * nodes[n]
-                    src1[t, r, m] = pltpu.roll(total, shifts[m], 1)
+                    dst1[t, 3, r, m] = pltpu.roll(total, shifts[m], 1)
                 for h in range(2):
                     for j in range(3):
                         first_hop(t, r, h, j).start()
 
                 @pl.when(side == 2)
                 def _():
-                    own_hop(t, r).start()
+                    for h in range(2):
+                        own_hop(t, r, h).start()
 
                 return carry
 
@@ -355,16 +358,15 @@
 
         @pl.when(t == 0)
         def _():
+            for copy in load_rest:
+                copy.wait()
+
             def first_slice(i, carry):
-                a = ordered(i)
-                for copy in load_slice(a):
-                    copy.wait()
-                in_face(a)
+                in_face(ordered(i))
                 return carry
 
             lax.fori_loop(1, N, first_slice, 0)
             lax.fori_loop(0, N, axial, 0)
-            load_scale.wait()
 
             @pl.when(is_mortar)
             def _():
@@ -380,7 +382,7 @@
 
                 lax.fori_loop(0, N, body, 0)
 
-        side_copy = hop(ap.at[fp], side_dst.at[t], side_send.at[t], side_recv.at[t], c, partner)
+        side_copy = hop(ap.at[fp], side_dst.at[t], side_send, side_recv.at[t % 2], c, partner)
         side_copy.start()
 
         def pack(a, carry):
@@ -395,25 +397,27 @@
         low, high = lax.fori_loop(0, N, pack, (zero, zero))
         halo_src[t, 0] = low
         halo_src[t, 1] = high
-        low_copy = hop(halo_src.at[t, 0], halo_dst.at[t, 0], halo_send.at[t, 0], halo_recv.at[t, 0], prv, side)
-        high_copy = hop(halo_src.at[t, 1], halo_dst.at[t, 1], halo_send.at[t, 1], halo_recv.at[t, 1], nxt, side)
+        low_copy = hop(halo_src.at[t, 0], halo_dst.at[t, 0], halo_send.at[0], halo_recv.at[t % 2, 0], prv, side)
+        high_copy = hop(halo_src.at[t, 1], halo_dst.at[t, 1], halo_send.at[1], halo_recv.at[t % 2, 1], nxt, side)
         low_copy.start()
         high_copy.start()
 
         @pl.when(is_relay)
         def _():
             def first_relay(r, carry):
-                @pl.when(side == 3)
-                def _():
-                    own_hop(t, r).wait_recv()
-
                 for h in range(2):
-                    for j in range(3):
-                        first_hop(t, r, h, j).wait_recv()
+                    @pl.when(side == 3)
+                    def _():
+                        landed(dst1.at[t, pl.ds(0, 4), r, nodes_of(h)], recv1.at[t % 2, r, h])
+
+                    @pl.when(side == 1)
+                    def _():
+                        landed(dst1.at[t, pl.ds(0, 3), r, nodes_of(h)], recv1.at[t % 2, r, h])
+
                     which = jnp.where(z_first(r, h), 0, 1)
                     for m in range(PIECES[h][0], sum(PIECES[h])):
                         src2[t, r, m] = pick(
-                            codes[t, which, m], src1[t, r, m], [dst1[t, j, r, m] for j in range(3)]
+                            codes[t, which, m], dst1[t, 3, r, m], [dst1[t, j, r, m] for j in range(3)]
                         )
                     for j in range(3):
                         second_hop(t, r, h, j).start()
@@ -456,8 +460,7 @@
             @pl.when(is_relay)
             def _():
                 for h in range(2):
-                    for j in range(3):
-                        second_hop(t, r, h, j).wait_recv()
+                    landed(dst2.at[t, pl.ds(0, 3), r, nodes_of(h)], recv2.at[t % 2, r, h])
                     which = jnp.where(z_first(r, h), 2, 0)
                     for m in range(PIECES[h][0], sum(PIECES[h])):
                         src3[t, r, m] = pick(
@@ -481,9 +484,7 @@
         @pl.when(is_mortar)
         def _():
             def arrive(r, carry):
-                for h in range(2):
-                    for j in range(2):
-                        last_hop(t, r, h, j).wait_recv()
+                landed(dst3.at[t, pl.ds(0, 2), r], recv3.at[t % 2, r])
                 nodes = [
                     jnp.where(codes[t, 3, m] == 0, dst3[t, 0, r, m], dst3[t, 1, r, m])
                     for m in range(N)
@@ -520,31 +521,20 @@
 
     lax.fori_loop(0, STEPS, step, 0)
 
-    def drain(i, carry):
-        t = i // N
-        r = i % N
-
-        @pl.when(is_mortar)
-        def _():
-            for h in range(2):
-                for j in range(3):
-                    first_hop(t, r, h, j).wait_send()
-
-        @pl.when(side == 2)
-        def _():
-            own_hop(t, r).wait_send()
-
-        @pl.when(is_relay)
-        def _():
-            for h in range(2):
-                for j in range(3):
-                    second_hop(t, r, h, j).wait_send()
-                for j in range(2):
-                    last_hop(t, r, h, j).wait_send()
-
-        return carry
-
-    lax.fori_loop(0, STEPS * N, drain, 0)
+    every = pl.ds(0, STEPS)
+
+    @pl.when(is_mortar)
+    def _():
+        sent(dst1.at[every, pl.ds(0, 3)], 0)
+
+    @pl.when(side == 2)
+    def _():
+        sent(dst1.at[every, 3], 1)
+
+    @pl.when(is_relay)
+    def _():
+        sent(dst2, 2)
+        sent(dst3, 3)
 
 
 def local(field, coeffs, reaction, step_scale, rotation):
@@ -577,27 +567,20 @@
             pltpu.VMEM((STEPS, 2, *tile), f32),
             pltpu.VMEM((STEPS, 2, *tile), f32),
             face_buffers(STEPS),
-            face_buffers(STEPS),
-            face_buffers(STEPS, 3),
+            face_buffers(STEPS, 4),
             face_buffers(STEPS),
             face_buffers(STEPS, 3),
             face_buffers(STEPS),
             face_buffers(STEPS, 2),
-            dma((N, 3)),
+            dma((7,)),
             dma((2,)),
+            dma((2, 2)),
             dma,
-            dma((STEPS, 2)),
-            dma((STEPS, 2)),
-            dma((STEPS,)),
-            dma((STEPS,)),
-            dma((STEPS, N)),
-            dma((STEPS, N)),
-            dma((STEPS, 3, N, 2)),
-            dma((STEPS, 3, N, 2)),
-            dma((STEPS, 3, N, 2)),
-            dma((STEPS, 3, N, 2)),
-            dma((STEPS, 2, N, 2)),
-            dma((STEPS, 2, N, 2)),
+            dma((2,)),
+            dma((4,)),
+            dma((2, N, 2)),
+            dma((2, N, 2)),
+            dma((2, N)),
         ],
         compiler_params=pltpu.CompilerParams(
             collective_id=0, has_side_effects=True, vmem_limit_bytes=61 * 1024 * 1024

time: 70 us -> 60.8 us (0.87)
  Pallas kernels: 68.8 us -> 59.6 us
    pallas_call x1, Pallas kernels: 68.8 us -> 59.6 us  [local(): pl.pallas_call(kernel, out_shape=pltpu.VMEM(block, f32), in_specs=[smem_s...]
where the time goes in v4:
time: 60.8 us; the launch traced here: 60.7 us
  Pallas kernels  59.6 us (98%)
  local copies, waits for them, and re-layouts  1.09 us (2%)
    pallas_call x1, Pallas kernels, local(): pl.pallas_call(kernel, out_shape=pltpu.VMEM(block, f32), in_specs=[smem_s...  59.6 us

profile of v4, /device:TPU:1, one launch (start us, length us, event | category | flops | bytes accessed | tf_op | source)
XLA Modules:
  0.0 60.7 jit_solution(11825307903180371484)
XLA Ops:
  0.0 59.6 %shard_map.64 = f32[7,7,7,8,128]{4,3,2,1,0:T(8,128)S(1)} custom-call(s32[4]{0:T(128)} %rot.1, f32[588]{0:T(1024)} %constant.2.clone.table, f32[7,7,7,8,128]{4,3,2,1,0:T(8,128)} %bitcast.7, f32[3,7,7,7,8,128]{5,4,3,2,1,0:T(8,128)} %bitcast.6, f32[7,7,7,8,128]{4,3,2,1,0:T(8,128)} %bitcast.8, f32[7,7,7,8,128]{4,3,2,1,0:T(8,128)} %bitcast.9), custom_call_target="tpu_custom_call" | custom-call | tf_op jit(solution)/shard_map/pallas_call | solution.py:552
  59.6 1.1 %copy.8 = f32[1,7,7,7,8,128]{5,4,3,2,1,0:T(8,128)} copy(f32[1,7,7,7,8,128]{5,4,3,2,1,0:T(8,128)S(1)} %bitcast.5) | data formatting | bytes 2809856

commit v5 on v4

--- a/solution.py
+++ b/solution.py
@@ -248,8 +248,7 @@
     in_face(fm)
     load_axial.wait()
 
-    @pl.when(is_mortar)
-    def _():
+    def first_face():
         def body(r, carry):
             for cc in range(N):
                 grad = half_line(DERIV, [u[a, r, cc] for a in range(N)])
@@ -260,6 +259,10 @@
             return carry
 
         lax.fori_loop(0, N, body, 0)
+
+    @pl.when(is_mortar)
+    def _():
+        first_face()
 
     def meet(which):
         @pl.when(side == which)
@@ -342,31 +345,10 @@
 
             lax.fori_loop(0, N, send, 0)
 
-            @pl.when(t > 0)
-            def _():
-                def rest(r, carry):
-                    for cc in range(N):
-                        d = delta[r, cc]
-                        res = half_line(DERIV.T, [(edge[p] * d) * co[0, p, r, cc] for p in range(N)])
-                        for a in range(N):
-                            ap[a, r, cc] = ap[a, r, cc] + res[a]
-                    for cc in range(N):
-                        ap[fm, r, cc] = face[r, cc]
-                    return carry
-
-                lax.fori_loop(0, N, rest, 0)
-
         @pl.when(t == 0)
         def _():
             for copy in load_rest:
                 copy.wait()
-
-            def first_slice(i, carry):
-                in_face(ordered(i))
-                return carry
-
-            lax.fori_loop(1, N, first_slice, 0)
-            lax.fori_loop(0, N, axial, 0)
 
             @pl.when(is_mortar)
             def _():
@@ -382,6 +364,9 @@
 
                 lax.fori_loop(0, N, body, 0)
 
+        lax.fori_loop(0, N, next_slice, 0)
+        lax.fori_loop(0, N, axial, 0)
+
         side_copy = hop(ap.at[fp], side_dst.at[t], side_send, side_recv.at[t % 2], c, partner)
         side_copy.start()
 
@@ -424,6 +409,23 @@
                 return carry
 
             lax.fori_loop(0, N, first_relay, 0)
+
+        def relay(r, carry):
+            @pl.when(is_relay)
+            def _():
+                for h in range(2):
+                    landed(dst2.at[t, pl.ds(0, 3), r, nodes_of(h)], recv2.at[t % 2, r, h])
+                    which = jnp.where(z_first(r, h), 2, 0)
+                    for m in range(PIECES[h][0], sum(PIECES[h])):
+                        src3[t, r, m] = pick(
+                            codes[t, which, m], src2[t, r, m], [dst2[t, j, r, m] for j in range(3)]
+                        )
+                    for j in range(2):
+                        last_hop(t, r, h, j).start()
+
+            return carry
+
+        lax.fori_loop(0, N, relay, 0)
 
         low_copy.wait()
         high_copy.wait()
@@ -456,30 +458,11 @@
 
         lax.fori_loop(0, N, add_side, 0)
 
-        def relay(r, carry):
-            @pl.when(is_relay)
-            def _():
-                for h in range(2):
-                    landed(dst2.at[t, pl.ds(0, 3), r, nodes_of(h)], recv2.at[t % 2, r, h])
-                    which = jnp.where(z_first(r, h), 2, 0)
-                    for m in range(PIECES[h][0], sum(PIECES[h])):
-                        src3[t, r, m] = pick(
-                            codes[t, which, m], src2[t, r, m], [dst2[t, j, r, m] for j in range(3)]
-                        )
-                    for j in range(2):
-                        last_hop(t, r, h, j).start()
-
-            @pl.when(t < STEPS - 1)
-            def _():
-                in_face(r)
-
-            return carry
-
-        lax.fori_loop(0, N, relay, 0)
-
-        @pl.when(t < STEPS - 1)
-        def _():
-            lax.fori_loop(0, N, axial, 0)
+
+        @pl.when(is_mortar & (t < STEPS - 1))
+        def _():
+            in_face(fm)
+            first_face()
 
         @pl.when(is_mortar)
         def _():
@@ -503,7 +486,7 @@
                 def _():
                     res = apply_line(changes, [co[2, fm, r, p] for p in range(N)])
                     for n in range(N):
-                        face[r, n] = ap[fm, r, n] + res[n] + diag[r, n] * changes[n]
+                        face[r, n] = face[r, n] + res[n] + diag[r, n] * changes[n]
 
                 return carry
 

time: 60.8 us -> 58.2 us (0.957)
  Pallas kernels: 59.6 us -> 57 us
    pallas_call x1, Pallas kernels: 59.6 us -> 57 us  [local(): pl.pallas_call(kernel, out_shape=pltpu.VMEM(block, f32), in_specs=[smem_s...]
where the time goes in v5:
time: 58.2 us; the launch traced here: 58.1 us
  Pallas kernels  57 us (98%)
  local copies, waits for them, and re-layouts  1.09 us (2%)
    pallas_call x1, Pallas kernels, local(): pl.pallas_call(kernel, out_shape=pltpu.VMEM(block, f32), in_specs=[smem_s...  57 us

profile of v5, /device:TPU:1, one launch (start us, length us, event | category | flops | bytes accessed | tf_op | source)
XLA Modules:
  0.0 58.1 jit_solution(5016601204588480768)
XLA Ops:
  0.0 57.0 %shard_map.64 = f32[7,7,7,8,128]{4,3,2,1,0:T(8,128)S(1)} custom-call(s32[4]{0:T(128)} %rot.1, f32[588]{0:T(1024)} %constant.2.clone.table, f32[7,7,7,8,128]{4,3,2,1,0:T(8,128)} %bitcast.7, f32[3,7,7,7,8,128]{5,4,3,2,1,0:T(8,128)} %bitcast.6, f32[7,7,7,8,128]{4,3,2,1,0:T(8,128)} %bitcast.8, f32[7,7,7,8,128]{4,3,2,1,0:T(8,128)} %bitcast.9), custom_call_target="tpu_custom_call" | custom-call | tf_op jit(solution)/shard_map/pallas_call | solution.py:535
  57.0 1.1 %copy.8 = f32[1,7,7,7,8,128]{5,4,3,2,1,0:T(8,128)} copy(f32[1,7,7,7,8,128]{5,4,3,2,1,0:T(8,128)S(1)} %bitcast.5) | data formatting | bytes 2809856

commit v6 on v5

--- a/solution.py
+++ b/solution.py
@@ -229,16 +229,24 @@
             for cc in range(N):
                 ap[a, r, cc] = ap[a, r, cc] + res[cc]
 
-    def axial(r, carry):
-        for cc in range(N):
+    def axial(r, columns):
+        for cc in columns:
             line = [u[a, r, cc] for a in range(N)]
             res = apply_line(line, [co[0, p, r, cc] for p in range(N)])
             for a in range(N):
                 ap[a, r, cc] = ap[a, r, cc] + res[a]
+
+        @pl.when(is_mortar)
+        def _():
+            for cc in columns:
+                ap[fm, r, cc] = face[r, cc]
+
+    def next_slice(i, carry):
+        in_face(ordered(i))
         return carry
 
-    def next_slice(a, carry):
-        in_face(a)
+    def ends(r, carry):
+        axial(r, (0, 6))
         return carry
 
     edge = [jnp.where(parity == 1, float(DERIV[p, 6]), float(DERIV[p, 0])) for p in range(N)]
@@ -364,11 +372,8 @@
 
                 lax.fori_loop(0, N, body, 0)
 
-        lax.fori_loop(0, N, next_slice, 0)
-        lax.fori_loop(0, N, axial, 0)
-
-        side_copy = hop(ap.at[fp], side_dst.at[t], side_send, side_recv.at[t % 2], c, partner)
-        side_copy.start()
+        lax.fori_loop(jnp.where(is_mortar, 1, 0), N, next_slice, 0)
+        lax.fori_loop(0, N, ends, 0)
 
         def pack(a, carry):
             low, high = carry
@@ -387,9 +392,9 @@
         low_copy.start()
         high_copy.start()
 
-        @pl.when(is_relay)
-        def _():
-            def first_relay(r, carry):
+        def first_relay(r, carry):
+            @pl.when(is_relay)
+            def _():
                 for h in range(2):
                     @pl.when(side == 3)
                     def _():
@@ -406,9 +411,14 @@
                         )
                     for j in range(3):
                         second_hop(t, r, h, j).start()
-                return carry
-
-            lax.fori_loop(0, N, first_relay, 0)
+
+            axial(r, (1, 2, 3, 4, 5))
+            return carry
+
+        lax.fori_loop(0, N, first_relay, 0)
+
+        side_copy = hop(ap.at[fp], side_dst.at[t], side_send, side_recv.at[t % 2], c, partner)
+        side_copy.start()
 
         def relay(r, carry):
             @pl.when(is_relay)

time: 58.2 us -> 56.5 us (0.971)
  Pallas kernels: 57 us -> 55.3 us
    pallas_call x1, Pallas kernels: 57 us -> 55.3 us  [local(): pl.pallas_call(kernel, out_shape=pltpu.VMEM(block, f32), in_specs=[smem_s...]
where the time goes in v6:
time: 56.5 us; the launch traced here: 56.4 us
  Pallas kernels  55.3 us (98%)
  local copies, waits for them, and re-layouts  1.09 us (2%)
    pallas_call x1, Pallas kernels, local(): pl.pallas_call(kernel, out_shape=pltpu.VMEM(block, f32), in_specs=[smem_s...  55.3 us

profile of v6, /device:TPU:1, one launch (start us, length us, event | category | flops | bytes accessed | tf_op | source)
XLA Modules:
  0.0 56.4 jit_solution(3455982880219197860)
XLA Ops:
  0.0 55.3 %shard_map.64 = f32[7,7,7,8,128]{4,3,2,1,0:T(8,128)S(1)} custom-call(s32[4]{0:T(128)} %rot.1, f32[588]{0:T(1024)} %constant.2.clone.table, f32[7,7,7,8,128]{4,3,2,1,0:T(8,128)} %bitcast.7, f32[3,7,7,7,8,128]{5,4,3,2,1,0:T(8,128)} %bitcast.6, f32[7,7,7,8,128]{4,3,2,1,0:T(8,128)} %bitcast.8, f32[7,7,7,8,128]{4,3,2,1,0:T(8,128)} %bitcast.9), custom_call_target="tpu_custom_call" | custom-call | tf_op jit(solution)/shard_map/pallas_call | solution.py:545
  55.3 1.1 %copy.8 = f32[1,7,7,7,8,128]{5,4,3,2,1,0:T(8,128)} copy(f32[1,7,7,7,8,128]{5,4,3,2,1,0:T(8,128)S(1)} %bitcast.5) | data formatting | bytes 2809856

commit v7 on v6

--- a/solution.py
+++ b/solution.py
@@ -165,10 +165,11 @@
 
     ring = z_dev + y_dev
     peers = {
-        1: [(d, 1) for d in ring] + [(d, 2) for d in x_dev] + [(d, 3) for d in x_dev],
-        2: [(d, 3) for d in ring] + [(d, 1) for d in x_dev],
-        3: [(d, 2) for d in ring] + [(d, 3) for d in ring] + [(d, 1) for d in x_dev],
+        1: [(d, 1) for d in ring] + [(d, 3) for d in x_dev],
+        2: [(d, 1) for d in x_dev],
+        3: [(d, 2) for d in ring] + [(d, 3) for d in ring],
     }
+    targets = {0: 3, 1: 3 + 6 + 2, 2: 3 + 6, 3: 3 + 6 + 2}
 
     def greet_peers(which):
         @pl.when(side == which)
@@ -275,7 +276,7 @@
     def meet(which):
         @pl.when(side == which)
         def _():
-            pl.semaphore_wait(barrier, 3 + len(peers.get(which, [])))
+            pl.semaphore_wait(barrier, targets[which])
 
     for which in range(4):
         meet(which)
@@ -295,16 +296,16 @@
     def first_hop(t, r, h, j):
         dev = jnp.where(z_first(r, h), z_dev[j], y_dev[j])
         return hop(dst1.at[t, 3, r, nodes_of(h)], dst1.at[t, j, r, nodes_of(h)],
-                   sends.at[0], recv1.at[t % 2, r, h], dev, first_side)
+                   sends.at[0], recv1.at[t % 2, r], dev, first_side)
 
     def own_hop(t, r, h):
         return hop(dst1.at[t, 3, r, nodes_of(h)], dst1.at[t, 3, r, nodes_of(h)],
-                   sends.at[1], recv1.at[t % 2, r, h], c, partner)
+                   sends.at[1], recv1.at[t % 2, r], c, partner)
 
     def second_hop(t, r, h, j):
         dev = jnp.where(z_first(r, h), y_dev[j], z_dev[j])
         return hop(src2.at[t, r, nodes_of(h)], dst2.at[t, j, r, nodes_of(h)],
-                   sends.at[2], recv2.at[t % 2, r, h], dev, side)
+                   sends.at[2], recv2.at[t % 2, r], dev, side)
 
     def last_hop(t, r, h, j):
         return hop(src3.at[t, r, nodes_of(h)], dst3.at[t, j, r, nodes_of(h)],
@@ -341,7 +342,7 @@
                         total = total + splat[t, m * N + n] * nodes[n]
                     dst1[t, 3, r, m] = pltpu.roll(total, shifts[m], 1)
                 for h in range(2):
-                    for j in range(3):
+                    for j in (1, 0, 2):
                         first_hop(t, r, h, j).start()
 
                 @pl.when(side == 2)
@@ -395,21 +396,21 @@
         def first_relay(r, carry):
             @pl.when(is_relay)
             def _():
+                @pl.when(side == 3)
+                def _():
+                    landed(dst1.at[t, pl.ds(0, 4), r], recv1.at[t % 2, r])
+
+                @pl.when(side == 1)
+                def _():
+                    landed(dst1.at[t, pl.ds(0, 3), r], recv1.at[t % 2, r])
+
                 for h in range(2):
-                    @pl.when(side == 3)
-                    def _():
-                        landed(dst1.at[t, pl.ds(0, 4), r, nodes_of(h)], recv1.at[t % 2, r, h])
-
-                    @pl.when(side == 1)
-                    def _():
-                        landed(dst1.at[t, pl.ds(0, 3), r, nodes_of(h)], recv1.at[t % 2, r, h])
-
                     which = jnp.where(z_first(r, h), 0, 1)
                     for m in range(PIECES[h][0], sum(PIECES[h])):
                         src2[t, r, m] = pick(
                             codes[t, which, m], dst1[t, 3, r, m], [dst1[t, j, r, m] for j in range(3)]
                         )
-                    for j in range(3):
+                    for j in (1, 0, 2):
                         second_hop(t, r, h, j).start()
 
             axial(r, (1, 2, 3, 4, 5))
@@ -423,8 +424,8 @@
         def relay(r, carry):
             @pl.when(is_relay)
             def _():
+                landed(dst2.at[t, pl.ds(0, 3), r], recv2.at[t % 2, r])
                 for h in range(2):
-                    landed(dst2.at[t, pl.ds(0, 3), r, nodes_of(h)], recv2.at[t % 2, r, h])
                     which = jnp.where(z_first(r, h), 2, 0)
                     for m in range(PIECES[h][0], sum(PIECES[h])):
                         src3[t, r, m] = pick(
@@ -571,8 +572,8 @@
             dma,
             dma((2,)),
             dma((4,)),
-            dma((2, N, 2)),
-            dma((2, N, 2)),
+            dma((2, N)),
+            dma((2, N)),
             dma((2, N)),
         ],
         compiler_params=pltpu.CompilerParams(

time: 56.5 us -> 55.7 us (0.986)
  Pallas kernels: 55.3 us -> 54.5 us
    pallas_call x1, Pallas kernels: 55.3 us -> 54.5 us  [local(): pl.pallas_call(kernel, out_shape=pltpu.VMEM(block, f32), in_specs=[smem_s...]
where the time goes in v7:
time: 55.7 us; the launch traced here: 55.6 us
  Pallas kernels  54.5 us (98%)
  local copies, waits for them, and re-layouts  1.09 us (2%)
    pallas_call x1, Pallas kernels, local(): pl.pallas_call(kernel, out_shape=pltpu.VMEM(block, f32), in_specs=[smem_s...  54.5 us

profile of v7, /device:TPU:1, one launch (start us, length us, event | category | flops | bytes accessed | tf_op | source)
XLA Modules:
  0.0 55.6 jit_solution(6139593132698290106)
XLA Ops:
  0.0 54.5 %shard_map.64 = f32[7,7,7,8,128]{4,3,2,1,0:T(8,128)S(1)} custom-call(s32[4]{0:T(128)} %rot.1, f32[588]{0:T(1024)} %constant.2.clone.table, f32[7,7,7,8,128]{4,3,2,1,0:T(8,128)} %bitcast.7, f32[3,7,7,7,8,128]{5,4,3,2,1,0:T(8,128)} %bitcast.6, f32[7,7,7,8,128]{4,3,2,1,0:T(8,128)} %bitcast.8, f32[7,7,7,8,128]{4,3,2,1,0:T(8,128)} %bitcast.9), custom_call_target="tpu_custom_call" | custom-call | tf_op jit(solution)/shard_map/pallas_call | solution.py:546
  54.5 1.1 %copy.8 = f32[1,7,7,7,8,128]{5,4,3,2,1,0:T(8,128)} copy(f32[1,7,7,7,8,128]{5,4,3,2,1,0:T(8,128)S(1)} %bitcast.5) | data formatting | bytes 2809856

commit v8 on v7

--- a/solution.py
+++ b/solution.py
@@ -97,12 +97,12 @@
 
 
 def kernel(
-    rot, table, field, coeffs, reaction, scale, u,
+    rot_in, table_in, field, coeffs, reaction, scale, u,
     co, re, sc, ap, splat, codes, face, delta, diag,
     halo_src, halo_dst, side_dst,
     dst1, src2, dst2, src3, dst3,
     load_sem, halo_send, halo_recv, side_send, side_recv,
-    sends, recv1, recv2, recv3,
+    sends, recv1, recv2, recv3, rot, table,
 ):
     c = lax.axis_index("circ")
     side = lax.axis_index("side")
@@ -180,8 +180,11 @@
     for which in peers:
         greet_peers(which)
 
-    for copy in load_first + [load_axial] + load_rest:
+    load_small = [load(7, rot_in, rot), load(8, table_in, table)]
+    for copy in load_small + load_first + [load_axial] + load_rest:
         copy.start()
+    for copy in load_small:
+        copy.wait()
 
     def digits(shift):
         s = shift & 127
@@ -538,7 +541,6 @@
     dma = pltpu.SemaphoreType.DMA
     table = jnp.asarray(mortar_constants().reshape(-1))
     hbm_spec = pl.BlockSpec(memory_space=pltpu.HBM)
-    smem_spec = pl.BlockSpec(memory_space=pltpu.SMEM)
 
     def face_buffers(*lead):
         return pltpu.VMEM((*lead, N, N, *tile), f32)
@@ -546,7 +548,7 @@
     result = pl.pallas_call(
         kernel,
         out_shape=pltpu.VMEM(block, f32),
-        in_specs=[smem_spec, smem_spec, hbm_spec, hbm_spec, hbm_spec, hbm_spec],
+        in_specs=[hbm_spec, hbm_spec, hbm_spec, hbm_spec, hbm_spec, hbm_spec],
         out_specs=pl.BlockSpec(memory_space=pltpu.VMEM),
         scratch_shapes=[
             pltpu.VMEM((3, *block), f32),
@@ -566,7 +568,7 @@
             face_buffers(STEPS, 3),
             face_buffers(STEPS),
             face_buffers(STEPS, 2),
-            dma((7,)),
+            dma((9,)),
             dma((2,)),
             dma((2, 2)),
             dma,
@@ -575,6 +577,8 @@
             dma((2, N)),
             dma((2, N)),
             dma((2, N)),
+            pltpu.SMEM(rotation.shape, jnp.int32),
+            pltpu.SMEM(table.shape, f32),
         ],
         compiler_params=pltpu.CompilerParams(
             collective_id=0, has_side_effects=True, vmem_limit_bytes=61 * 1024 * 1024

time: 55.7 us -> 55.1 us (0.989)
  Pallas kernels: 54.5 us -> 53.9 us
where the time goes in v8:
time: 55.1 us; the launch traced here: 55 us
  Pallas kernels  53.9 us (98%)
  local copies, waits for them, and re-layouts  1.09 us (2%)
    pallas_call x1, Pallas kernels, local(): pl.pallas_call(kernel, out_shape=pltpu.VMEM(block, f32), in_specs=[hbm_sp...  53.9 us

profile of v8, /device:TPU:1, one launch (start us, length us, event | category | flops | bytes accessed | tf_op | source)
XLA Modules:
  0.0 55.0 jit_solution(11967164320047158148)
XLA Ops:
  0.0 53.9 %shard_map.64 = f32[7,7,7,8,128]{4,3,2,1,0:T(8,128)S(1)} custom-call(s32[4]{0:T(128)} %rot_in.1, f32[588]{0:T(1024)} %constant.2.clone.table_in, f32[7,7,7,8,128]{4,3,2,1,0:T(8,128)} %bitcast.7, f32[3,7,7,7,8,128]{5,4,3,2,1,0:T(8,128)} %bitcast.6, f32[7,7,7,8,128]{4,3,2,1,0:T(8,128)} %bitcast.8, f32[7,7,7,8,128]{4,3,2,1,0:T(8,128)} %bitcast.9), custom_call_target="tpu_custom_call" | custom-call | tf_op jit(solution)/shard_map/pallas_call | solution.py:548
  54.0 1.1 %copy.8 = f32[1,7,7,7,8,128]{5,4,3,2,1,0:T(8,128)} copy(f32[1,7,7,7,8,128]{5,4,3,2,1,0:T(8,128)S(1)} %bitcast.5) | data formatting | bytes 2809856

commit v9 on v8

--- a/solution.py
+++ b/solution.py
@@ -312,7 +312,7 @@
 
     def last_hop(t, r, h, j):
         return hop(src3.at[t, r, nodes_of(h)], dst3.at[t, j, r, nodes_of(h)],
-                   sends.at[3], recv3.at[t % 2, r], x_dev[j], last_side)
+                   sends.at[3], recv3.at[t % 2, r // 4], x_dev[j], last_side)
 
     def landed(ref, sem):
         hop(ref, ref, sends.at[0], sem, c, partner).wait_recv()
@@ -481,7 +481,6 @@
         @pl.when(is_mortar)
         def _():
             def arrive(r, carry):
-                landed(dst3.at[t, pl.ds(0, 2), r], recv3.at[t % 2, r])
                 nodes = [
                     jnp.where(codes[t, 3, m] == 0, dst3[t, 0, r, m], dst3[t, 1, r, m])
                     for m in range(N)
@@ -504,7 +503,10 @@
 
                 return carry
 
-            lax.fori_loop(0, N, arrive, 0)
+            landed(dst3.at[t, pl.ds(0, 2), pl.ds(0, 4)], recv3.at[t % 2, 0])
+            lax.fori_loop(0, 4, arrive, 0)
+            landed(dst3.at[t, pl.ds(0, 2), pl.ds(4, 3)], recv3.at[t % 2, 1])
+            lax.fori_loop(4, N, arrive, 0)
 
             @pl.when(t < STEPS - 1)
             def _():
@@ -576,7 +578,7 @@
             dma((4,)),
             dma((2, N)),
             dma((2, N)),
-            dma((2, N)),
+            dma((2, 2)),
             pltpu.SMEM(rotation.shape, jnp.int32),
             pltpu.SMEM(table.shape, f32),
         ],

time: 55.1 us -> 55.3 us (level)
  no operation moved by 1% of the time
where the time goes in v9:
time: 55.3 us; the launch traced here: 55.2 us
  Pallas kernels  54.1 us (98%)
  local copies, waits for them, and re-layouts  1.09 us (2%)
    pallas_call x1, Pallas kernels, local(): pl.pallas_call(kernel, out_shape=pltpu.VMEM(block, f32), in_specs=[hbm_sp...  54.1 us

profile of v9, /device:TPU:1, one launch (start us, length us, event | category | flops | bytes accessed | tf_op | source)
XLA Modules:
  0.0 55.2 jit_solution(1853528148173342199)
XLA Ops:
  0.0 54.1 %shard_map.64 = f32[7,7,7,8,128]{4,3,2,1,0:T(8,128)S(1)} custom-call(s32[4]{0:T(128)} %rot_in.1, f32[588]{0:T(1024)} %constant.2.clone.table_in, f32[7,7,7,8,128]{4,3,2,1,0:T(8,128)} %bitcast.7, f32[3,7,7,7,8,128]{5,4,3,2,1,0:T(8,128)} %bitcast.6, f32[7,7,7,8,128]{4,3,2,1,0:T(8,128)} %bitcast.8, f32[7,7,7,8,128]{4,3,2,1,0:T(8,128)} %bitcast.9), custom_call_target="tpu_custom_call" | custom-call | tf_op jit(solution)/shard_map/pallas_call | solution.py:550
  54.1 1.1 %copy.8 = f32[1,7,7,7,8,128]{5,4,3,2,1,0:T(8,128)} copy(f32[1,7,7,7,8,128]{5,4,3,2,1,0:T(8,128)S(1)} %bitcast.5) | data formatting | bytes 2809856
